TPU v7x, 32 devices: a whole 2x2x4 slice. The times are simulated.
32 devices in a mesh: row: 4 (over y, x), col: 8 (over z, core).
Axes of the slice: x: 2, y: 2, z: 4, core: 2. Of those that a mesh axis runs over, the one named last changes fastest.
Arguments:
- pair: float32 [256, 256, 128], P('row', 'col'), may hold values from -6 to 6
- valid_length: int32 [1], replicated, may hold values from 64 to 255
- tri_in: bfloat16 [128, 512], replicated, may hold values from -0.5 to 0.5
- tri_gate: bfloat16 [128, 128], replicated, may hold values from -0.5 to 0.5
- tri_out: bfloat16 [128, 128], replicated, may hold values from -0.5 to 0.5
- att_in: bfloat16 [128, 512], replicated, may hold values from -16.9705627 to 16.9705627
- att_bias: bfloat16 [128, 4], replicated, may hold values from -0.5 to 0.5
- att_out: bfloat16 [128, 128], replicated, may hold values from -0.5 to 0.5
Outputs:
- pair_out: float32 [256, 256, 128], P('row', 'col')
Inputs may be any that keep to these rules, and one draw needn't show every extreme that they name: Tokens at positions below valid_length[0] are real, the rest are padding.
All inputs are finite; a program needn't handle non-finite values.
Results may differ from a plain program's by a relative error of at most 0.025.
Values may be sent and summed in bfloat16 or wider, within the bound.
A program may use at most 128 MiB of HBM per device.

v0:
```python
import functools

import jax
import jax.numpy as jnp
from jax import lax
from jax.experimental import pallas as pl
from jax.experimental.pallas import tpu as pltpu
from jax.sharding import PartitionSpec as P

MESH = pl.DeviceIdType.MESH
F32 = jnp.float32
BF16 = jnp.bfloat16


def norm(values, axis):
    center = values - jnp.mean(values, axis=axis, keepdims=True)
    return center * lax.rsqrt(jnp.mean(center * center, axis=axis, keepdims=True) + 1e-05)


def swap_groups(blocks, lane, group):
    count = len(blocks)
    width = count * group
    out = []
    for b in range(count):
        total = None
        for a in range(count):
            shift = (group * (a - b)) % width
            moved = blocks[a] if shift == 0 else pltpu.roll(blocks[a], shift, 1)
            total = moved if total is None else jnp.where(lane == a, moved, total)
        out.append(total)
    return out


def kernel(
    dims,
    valid_ref, pair_ref, tri_in_ref, tri_gate_ref, tri_out_ref, att_in_ref, bias_w_ref, att_out_ref,
    out_ref,
    normed_s, edge_f, left_send, right_send, left_recv, right_recv, left_s, right_s,
    prod_send, prod_recv, prod_f, tri_gate_s, mid_send, mid_recv, qkv_s, gate_s,
    bias_f, bias_send, bias_recv, bias_full, gated_s, gated_recv,
    send_l, recv_l, send_r, recv_r, send_p, recv_p, send_m, recv_m, send_b, recv_b, send_c, recv_c,
    send_g, recv_g,
):
    nrow, ncol, rows_dev, cols_dev, width, heads = dims
    ndev = nrow * ncol
    total = ncol * cols_dev
    group = 128 // cols_dev
    tiles = rows_dev // group
    chans = width // ndev
    parts = 2 if chans % 2 == 0 else 1
    each = chans // parts
    per = rows_dev // ncol
    head_size = width // heads
    my_row, my_col = lax.axis_index("row"), lax.axis_index("col")
    me = my_row * ncol + my_col
    valid = valid_ref[0]

    def other(step):
        peer = lax.rem(me + step, ndev)
        return peer, (peer // ncol, lax.rem(peer, ncol))

    def loop(count, act):
        def run(step, carry):
            act(step)
            return carry

        lax.fori_loop(1, count, run, 0)

    barrier = pltpu.get_barrier_semaphore()
    loop(
        ndev,
        lambda step: pl.semaphore_signal(
            barrier, inc=1, device_id=other(step)[1], device_id_type=MESH
        ),
    )

    lanes = lax.broadcasted_iota(jnp.int32, (1, 128), 1)
    lane_col = my_col * cols_dev + lanes % cols_dev
    lane_row = my_row * rows_dev + (lanes // cols_dev) * tiles

    def edges(side):
        first = 2 * side * width
        for t in range(tiles):
            if side == 0:
                rows = jnp.concatenate([pair_ref[g * tiles + t] for g in range(group)], axis=0)
                normed_s[t] = norm(rows, 1).astype(BF16)
            proj = jnp.dot(
                normed_s[t], tri_in_ref[:, first : first + 2 * width], preferred_element_type=F32
            )
            keep = jnp.where((lane_row + t < valid) & (lane_col < valid), 1.0, 0.0)
            edge = jax.nn.sigmoid(proj[:, :width]) * proj[:, width:]
            edge_f[side, pl.ds(t, width, stride=tiles), :] = jnp.transpose(edge) * keep

    def pack(side, target):
        for c in range(chans):
            target[c] = edge_f[side, pl.ds(c * ndev * tiles, ndev * tiles), :].astype(BF16)

    def share(peer):
        return pl.ds(pl.multiple_of(peer * tiles, tiles), tiles)

    def left_copy(step):
        peer, where = other(step)
        return pltpu.make_async_remote_copy(
            src_ref=left_send.at[:, share(peer), :], dst_ref=left_recv.at[me],
            send_sem=send_l.at[step], recv_sem=recv_l.at[step],
            device_id=where, device_id_type=MESH,
        )

    def right_copy(part, step):
        peer, where = other(step)
        some = pl.ds(part * each, each)
        return pltpu.make_async_remote_copy(
            src_ref=right_send.at[some, share(peer), :], dst_ref=right_recv.at[me, some],
            send_sem=send_r.at[part, step], recv_sem=recv_r.at[part, step],
            device_id=where, device_id_type=MESH,
        )

    edges(0)
    pack(0, left_send)
    pl.semaphore_wait(barrier, ndev - 1)
    loop(ndev, lambda step: left_copy(step).start())
    edges(1)
    pack(1, right_send)
    for part in range(parts):
        loop(ndev, lambda step: right_copy(part, step).start())
    left_recv[me] = left_send[:, share(me), :]
    right_recv[me] = right_send[:, share(me), :]
    for t in range(tiles):
        tri_gate_s[t] = jax.nn.sigmoid(
            jnp.dot(normed_s[t], tri_gate_ref[...], preferred_element_type=F32)
        )
    loop(ndev, lambda step: left_copy(step).wait())

    lane = lax.broadcasted_iota(jnp.int32, (tiles, 128), 1) // cols_dev

    def spread(c, source, operand):
        for r in range(nrow):
            for half in range(ncol // group):
                blocks = [
                    source[r * ncol + half * group + a, c].astype(F32) for a in range(group)
                ]
                for b, piece in enumerate(swap_groups(blocks, lane, cols_dev)):
                    operand[
                        pl.ds(r * rows_dev + b * tiles, tiles), pl.ds(half * 128, 128)
                    ] = piece.astype(BF16)

    def prod_copy(part, step):
        peer, where = other(step)
        some = pl.ds(part * each, each)
        return pltpu.make_async_remote_copy(
            src_ref=prod_send.at[peer, some], dst_ref=prod_recv.at[me, some],
            send_sem=send_p.at[part, step], recv_sem=recv_p.at[part, step],
            device_id=where, device_id_type=MESH,
        )

    for c in range(chans):
        spread(c, left_recv, left_s.at[c])
    for part in range(parts):
        loop(ndev, lambda step: right_copy(part, step).wait())
        for c in range(part * each, (part + 1) * each):
            spread(c, right_recv, right_s.at[c])
            products = lax.dot_general(
                left_s[c], right_s[c], (((1,), (1,)), ((), ())), preferred_element_type=F32
            )
            for r in range(nrow):
                for half in range(ncol // group):
                    blocks = [
                        products[
                            r * rows_dev + a * tiles : r * rows_dev + (a + 1) * tiles,
                            half * 128 : (half + 1) * 128,
                        ]
                        for a in range(group)
                    ]
                    for b, piece in enumerate(swap_groups(blocks, lane, cols_dev)):
                        prod_send[r * ncol + half * group + b, c] = piece.astype(BF16)
        loop(ndev, lambda step: prod_copy(part, step).start())
    prod_recv[me] = prod_send[me]

    for part in range(parts):
        loop(ndev, lambda step: prod_copy(part, step).wait())
        for c in range(part * each, (part + 1) * each):
            for d in range(ndev):
                prod_f[pl.ds((c * ndev + d) * tiles, tiles), :] = prod_recv[d, c].astype(F32)

    def strip(peer):
        return pl.ds(pl.multiple_of(peer * cols_dev, cols_dev), cols_dev)

    def mid_copy(i, step):
        peer = lax.rem(my_col + step, ncol)
        return pltpu.make_async_remote_copy(
            src_ref=mid_send.at[i, peer], dst_ref=mid_recv.at[i, strip(my_col), :],
            send_sem=send_m.at[i, step], recv_sem=recv_m.at[i, step],
            device_id=(my_row, peer), device_id_type=MESH,
        )

    for i in range(per):
        for t in range(i, tiles, per):
            prods = norm(prod_f[pl.ds(t, width, stride=tiles), :], 0)
            prods = jnp.transpose(prods).astype(BF16)
            update = jnp.dot(prods, tri_out_ref[...], preferred_element_type=F32)
            rows = jnp.concatenate([pair_ref[g * tiles + t] for g in range(group)], axis=0)
            middle = rows + tri_gate_s[t] * update
            normed_mid = norm(middle, 1).astype(BF16)
            for g in range(group):
                row = g * tiles + t
                out_ref[row] = middle[g * cols_dev : (g + 1) * cols_dev]
                mid_send[i, row // per] = normed_mid[g * cols_dev : (g + 1) * cols_dev]
        for step in range(1, ncol):
            mid_copy(i, step).start()
        mid_recv[i, strip(my_col), :] = mid_send[i, my_col]

    for i in range(per):
        for step in range(1, ncol):
            mid_copy(i, step).wait()
        own = lax.dot_general(
            bias_w_ref[...], mid_recv[i], (((1,), (1,)), ((), ())), preferred_element_type=F32
        )
        for h in range(heads):
            bias_f[pl.ds(h * per + i, 1), :] = own[h : h + 1]
        if i < per - 1:
            project(i, mid_recv, att_in_ref, qkv_s, gate_s, width, head_size)
    bias_send[...] = bias_f[...].astype(BF16)

    side = lax.rem(my_col, 2)
    mine = me // 2

    def bias_copy(step):
        peer = 2 * lax.rem(mine + step, ndev // 2) + side
        return pltpu.make_async_remote_copy(
            src_ref=bias_send, dst_ref=bias_recv.at[side, mine],
            send_sem=send_b.at[step], recv_sem=recv_b.at[step],
            device_id=(peer // ncol, lax.rem(peer, ncol)), device_id_type=MESH,
        )

    loop(ndev // 2, lambda step: bias_copy(step).start())
    bias_recv[side, mine] = bias_send[...]
    project(per - 1, mid_recv, att_in_ref, qkv_s, gate_s, width, head_size)
    loop(ndev // 2, lambda step: bias_copy(step).wait())
    hand = pltpu.make_async_remote_copy(
        src_ref=bias_recv.at[side], dst_ref=bias_recv.at[side],
        send_sem=send_c, recv_sem=recv_c,
        device_id=(my_row, my_col + 1 - 2 * side), device_id_type=MESH,
    )
    hand.start()
    hand.wait()
    tokens = lax.broadcasted_iota(jnp.int32, (1, total), 1)
    mask = jnp.where(tokens < valid, 0.0, -1000000000.0)
    for d in range(ndev):
        piece = bias_recv[d % 2, d // 2].astype(F32) + mask
        for h in range(heads):
            bias_full[h, pl.ds(d * per, per), :] = piece[h * per : (h + 1) * per]

    block = 128
    head = lax.broadcasted_iota(jnp.int32, (block, width), 1) // head_size

    def home_copy(i, step):
        peer = lax.rem(my_col + step, ncol)
        return pltpu.make_async_remote_copy(
            src_ref=gated_s.at[i, strip(peer), :], dst_ref=gated_recv.at[i, strip(my_col), :],
            send_sem=send_g.at[i, step], recv_sem=recv_g.at[i, step],
            device_id=(my_row, peer), device_id_type=MESH,
        )

    def attend(i, carry):
        keys = qkv_s[i, :, width : 2 * width]
        values = jnp.concatenate(
            [qkv_s[i, :, 2 * width : 3 * width], jnp.ones((total, width), BF16)], axis=1
        )
        for first in range(0, total, block):
            query = qkv_s[i, first : first + block, :width]
            top = jnp.zeros((block, width), F32)
            bottom = jnp.ones((block, width), F32)
            for h in range(heads):
                scores = lax.dot_general(
                    jnp.where(head == h, query, jnp.zeros_like(query)), keys,
                    (((1,), (1,)), ((), ())), preferred_element_type=F32,
                )
                scores = scores + bias_full[h, first : first + block, :]
                expo = jnp.exp(scores - jnp.max(scores, axis=1, keepdims=True)).astype(BF16)
                both = jnp.dot(expo, values, preferred_element_type=F32)
                top = jnp.where(head == h, both[:, :width], top)
                bottom = jnp.where(head == h, both[:, width:], bottom)
            gated_s[i, first : first + block, :] = (
                gate_s[i, first : first + block, :] * top / bottom
            ).astype(BF16)
        for step in range(1, ncol):
            home_copy(i, step).start()
        gated_recv[i, strip(my_col), :] = gated_s[i, strip(my_col), :]
        return carry

    lax.fori_loop(0, per, attend, 0)

    def finish(i, carry):
        for step in range(1, ncol):
            home_copy(i, step).wait()
        added = jnp.dot(gated_recv[i], att_out_ref[...], preferred_element_type=F32)
        for q in range(ncol):
            out_ref[q * per + i] += added[q * cols_dev : (q + 1) * cols_dev]
        return carry

    lax.fori_loop(0, per, finish, 0)


def project(i, mid_recv, att_in_ref, qkv_s, gate_s, width, head_size):
    proj = jnp.dot(mid_recv[i], att_in_ref[...], preferred_element_type=F32)
    qkv_s[i, :, :width] = (proj[:, :width] * head_size ** (-0.5)).astype(BF16)
    qkv_s[i, :, width : 3 * width] = proj[:, width : 3 * width].astype(BF16)
    gate_s[i] = jax.nn.sigmoid(proj[:, 3 * width :])


def per_device(pair, valid_length, tri_in, tri_gate, tri_out, att_in, att_bias, att_out):
    rows_dev, cols_dev, width = pair.shape
    heads = att_bias.shape[1]
    nrow, ncol = lax.axis_size("row"), lax.axis_size("col")
    ndev = nrow * ncol
    total = ncol * cols_dev
    tiles = rows_dev // (128 // cols_dev)
    chans = width // ndev
    parts = 2 if chans % 2 == 0 else 1
    per = rows_dev // ncol
    vmem = pl.BlockSpec(memory_space=pltpu.VMEM)
    sems = lambda *shape: [pltpu.SemaphoreType.DMA(shape)] * 2
    held = lambda dtype, *shape: pltpu.VMEM(shape, dtype)
    return pl.pallas_call(
        functools.partial(kernel, (nrow, ncol, rows_dev, cols_dev, width, heads)),
        out_shape=jax.ShapeDtypeStruct((rows_dev, cols_dev, width), F32),
        in_specs=[pl.BlockSpec(memory_space=pltpu.SMEM)] + [vmem] * 7,
        out_specs=vmem,
        scratch_shapes=[
            held(BF16, tiles, 128, width),
            held(F32, 2, width * tiles, 128),
            held(BF16, chans, ndev * tiles, 128),
            held(BF16, chans, ndev * tiles, 128),
            held(BF16, ndev, chans, tiles, 128),
            held(BF16, ndev, chans, tiles, 128),
            held(BF16, chans, total, total),
            held(BF16, chans, total, total),
            held(BF16, ndev, chans, tiles, 128),
            held(BF16, ndev, chans, tiles, 128),
            held(F32, width * tiles, 128),
            held(F32, tiles, 128, width),
            held(BF16, per, ncol, cols_dev, width),
            held(BF16, per, total, width),
            held(BF16, per, total, 3 * width),
            held(F32, per, total, width),
            held(F32, heads * per, total),
            held(BF16, heads * per, total),
            held(BF16, 2, ndev // 2, heads * per, total),
            held(F32, heads, total, total),
            held(BF16, per, total, width),
            held(BF16, per, total, width),
            *sems(ndev), *sems(parts, ndev), *sems(parts, ndev), *sems(per, ncol), *sems(ndev // 2),
            pltpu.SemaphoreType.DMA, pltpu.SemaphoreType.DMA,
            *sems(per, ncol),
        ],
        compiler_params=pltpu.CompilerParams(
            collective_id=0, has_side_effects=True, vmem_limit_bytes=56 * 1024 * 1024
        ),
    )(valid_length, pair, tri_in, tri_gate, tri_out, att_in, att_bias.T, att_out)


def solution(mesh):
    placed = (P("row", "col", None), P(), P(), P(), P(), P(), P(), P())
    return jax.shard_map(
        per_device, mesh=mesh, in_specs=placed, out_specs=P("row", "col", None), check_vma=False
    )
```

profile of v0, /device:TPU:0, one launch (start us, length us, event | category | flops | bytes accessed | tf_op | source)
XLA Modules:
  0.0 90.9 jit_solution(5414853418191989328)
XLA Ops:
  0.7 88.0 %shard_map.82 = f32[64,32,128]{2,1,0:T(8,128)} custom-call(s32[1]{0:T(128)S(6)} %copy.10.valid_ref, f32[64,32,128]{2,1,0:T(8,128)} %pair_ref.1, bf16[128,512]{1,0:T(8,128)(2,1)} %tri_in_ref.1, bf16[128,128]{1,0:T(8,128)(2,1)} %tri_gate_ref.1, bf16[128,128]{1,0:T(8,128)(2,1)} %tri_out_ref.1, bf16[128,512]{1,0:T(8,128)(2,1)} %att_in_ref.1, ...), custom_call_target="tpu_custom_call" | custom-call | tf_op jit(solution)/shard_map/pallas_call | solution.py:324
  88.7 2.3 %copy.11 = f32[64,32,128]{2,1,0:T(8,128)} copy(f32[64,32,128]{2,1,0:T(8,128)} %shard_map.82) | data formatting | bytes 2097152
where the time goes:
time: 91.1 us; the launch traced here: 90.9 us
  Pallas kernels  88 us (97%)
  local copies, waits for them, and re-layouts  2.26 us (2%)
    pallas_call x1, Pallas kernels, per_device(): pl.pallas_call(functools.partial(kernel, (nrow, ncol, rows_dev, cols_dev,...  88 us
    unnamed x1, local copies, waits for them, and re-layouts  2.26 us

commit v1 on v0

v1 whole, which is shorter than its diff:
```python
import functools

import jax
import jax.numpy as jnp
from jax import lax
from jax.experimental import pallas as pl
from jax.experimental.pallas import tpu as pltpu
from jax.sharding import PartitionSpec as P

MESH = pl.DeviceIdType.MESH
F32 = jnp.float32
BF16 = jnp.bfloat16
scope = jax.named_scope


def norm(values, axis):
    center = values - jnp.mean(values, axis=axis, keepdims=True)
    return center * lax.rsqrt(jnp.mean(center * center, axis=axis, keepdims=True) + 1e-05)


def swap_groups(blocks, lane, group):
    count = len(blocks)
    width = count * group
    out = []
    for b in range(count):
        total = None
        for a in range(count):
            shift = (group * (a - b)) % width
            moved = blocks[a] if shift == 0 else pltpu.roll(blocks[a], shift, 1)
            total = moved if total is None else jnp.where(lane == a, moved, total)
        out.append(total)
    return out


def arrived(ref, sem):
    pltpu.make_async_copy(ref, ref, sem).wait()


def kernel(
    dims,
    valid_ref, pair_h, tri_in_h, tri_gate_h, tri_out_h, att_in_h, bias_w_h, att_out_h,
    out_ref,
    pair_ref, tri_in_ref, tri_gate_ref, tri_out_ref, att_in_ref, bias_w_ref, att_out_ref,
    normed_s, edge_f, left_send, right_send, left_recv, right_recv, left_s, right_s,
    prod_send, prod_recv, prod_f, tri_gate_s, mid_send, mid_recv, qkv_s, gate_s,
    bias_f, bias_recv, bias_full, gated_s, gated_recv,
    sem_in, send_l, recv_l, send_r, recv_r, send_p, recv_p, send_m, recv_m,
    send_b, recv_b, send_g, recv_g,
):
    nrow, ncol, rows_dev, cols_dev, width, heads, parts, halves = dims
    ndev = nrow * ncol
    total = ncol * cols_dev
    group = 128 // cols_dev
    tiles = rows_dev // group
    chans = width // ndev
    each = chans // parts
    per = rows_dev // ncol
    high = tiles // halves
    nz = ncol // 2
    head_size = width // heads
    my_row, my_col = lax.axis_index("row"), lax.axis_index("col")
    me = my_row * ncol + my_col
    core, my_z = lax.rem(my_col, 2), my_col // 2

    held = (pair_ref, tri_in_ref, tri_gate_ref, tri_out_ref, att_in_ref, bias_w_ref, att_out_ref)
    given = (pair_h, tri_in_h, tri_gate_h, tri_out_h, att_in_h, bias_w_h, att_out_h)
    loads = [pltpu.make_async_copy(g, v, sem_in.at[k]) for k, (g, v) in enumerate(zip(given, held))]
    for k in (0, 1, 2, 3, 5, 4, 6):
        loads[k].start()

    def other(step):
        peer = lax.rem(me + step, ndev)
        return peer, (peer // ncol, lax.rem(peer, ncol))

    def loop(count, act):
        def run(step, carry):
            act(step)
            return carry

        lax.fori_loop(1, count, run, 0)

    with scope("signal"):
        barrier = pltpu.get_barrier_semaphore()
        loop(
            ndev,
            lambda step: pl.semaphore_signal(
                barrier, inc=1, device_id=other(step)[1], device_id_type=MESH
            ),
        )
    with scope("inputs"):
        for k in (0, 1):
            loads[k].wait()
    valid = valid_ref[0]

    lanes = lax.broadcasted_iota(jnp.int32, (1, 128), 1)
    lane_col = my_col * cols_dev + lanes % cols_dev
    lane_row = my_row * rows_dev + (lanes // cols_dev) * tiles

    def edges(side):
        first = 2 * side * width
        for t in range(tiles):
            if side == 0:
                rows = jnp.concatenate([pair_ref[g * tiles + t] for g in range(group)], axis=0)
                normed_s[t] = norm(rows, 1).astype(BF16)
            proj = jnp.dot(
                normed_s[t], tri_in_ref[:, first : first + 2 * width], preferred_element_type=F32
            )
            keep = jnp.where((lane_row + t < valid) & (lane_col < valid), 1.0, 0.0)
            edge = jax.nn.sigmoid(proj[:, :width]) * proj[:, width:]
            edge_f[side, pl.ds(t, width, stride=tiles), :] = jnp.transpose(edge) * keep

    def pack(side, target):
        for c in range(chans):
            target[c] = edge_f[side, pl.ds(c * ndev * tiles, ndev * tiles), :].astype(BF16)

    def share(peer):
        return pl.ds(pl.multiple_of(peer * tiles, tiles), tiles)

    def remote(src, dst, send, recv, where):
        return pltpu.make_async_remote_copy(
            src_ref=src, dst_ref=dst, send_sem=send, recv_sem=recv, device_id=where, device_id_type=MESH
        )

    def left_copy(step):
        peer, where = other(step)
        return remote(left_send.at[:, share(peer), :], left_recv.at[me], send_l, recv_l, where)

    def right_copy(part, step):
        peer, where = other(step)
        some = pl.ds(part * each, each)
        return remote(
            right_send.at[some, share(peer), :], right_recv.at[part, me],
            send_r.at[part], recv_r.at[part], where,
        )

    with scope("edges0"):
        edges(0)
        pack(0, left_send)
    with scope("barrier"):
        pl.semaphore_wait(barrier, ndev - 1)
    with scope("sendl"):
        loop(ndev, lambda step: left_copy(step).start())
    with scope("edges1"):
        edges(1)
        pack(1, right_send)
    with scope("sendr"):
        for part in range(parts):
            loop(ndev, lambda step: right_copy(part, step).start())
    with scope("gate"):
        left_recv[me] = left_send[:, share(me), :]
        for part in range(parts):
            right_recv[part, me] = right_send[part * each : (part + 1) * each, share(me), :]
        for k in (2, 3, 5, 4, 6):
            loads[k].wait()
        for t in range(tiles):
            tri_gate_s[t] = jax.nn.sigmoid(
                jnp.dot(normed_s[t], tri_gate_ref[...], preferred_element_type=F32)
            )
    others = pl.ds(0, ndev - 1)
    with scope("waitl"):
        arrived(left_recv.at[others], recv_l)

    lane = lax.broadcasted_iota(jnp.int32, (tiles, 128), 1) // cols_dev

    def spread(load, operand):
        for r in range(nrow):
            for half in range(ncol // group):
                blocks = [load(r * ncol + half * group + a).astype(F32) for a in range(group)]
                for b, piece in enumerate(swap_groups(blocks, lane, cols_dev)):
                    operand[
                        pl.ds(r * rows_dev + b * tiles, tiles), pl.ds(half * 128, 128)
                    ] = piece.astype(BF16)

    def prod_copy(part, hh, step):
        peer, where = other(step)
        some = pl.ds(part * each * high, each * high)
        return remote(
            prod_send.at[peer, hh, some], prod_recv.at[hh, part, me],
            send_p.at[part, hh], recv_p.at[part, hh], where,
        )

    with scope("spreadl"):
        for c in range(chans):
            spread(lambda d: left_recv[d, c], left_s.at[c])
    for part in range(parts):
        with scope("waitr"):
            arrived(right_recv.at[part, others], recv_r.at[part])
        with scope("products"):
            for c in range(part * each, (part + 1) * each):
                spread(lambda d: right_recv[part, d, c - part * each], right_s.at[c])
                products = lax.dot_general(
                    left_s[c], right_s[c], (((1,), (1,)), ((), ())), preferred_element_type=F32
                )
                for r in range(nrow):
                    for half in range(ncol // group):
                        blocks = [
                            products[
                                r * rows_dev + a * tiles : r * rows_dev + (a + 1) * tiles,
                                half * 128 : (half + 1) * 128,
                            ]
                            for a in range(group)
                        ]
                        for b, piece in enumerate(swap_groups(blocks, lane, cols_dev)):
                            for hh in range(halves):
                                prod_send[r * ncol + half * group + b, hh, c * high : (c + 1) * high] = piece[
                                    hh * high : (hh + 1) * high
                                ].astype(BF16)
        with scope("sendp"):
            for hh in range(halves):
                loop(ndev, lambda step: prod_copy(part, hh, step).start())
                prod_recv[hh, part, me] = prod_send[me, hh, part * each * high : (part + 1) * each * high]

    def strip(peer):
        return pl.ds(pl.multiple_of(peer * cols_dev, cols_dev), cols_dev)

    def send_rows(t):
        i = t % per
        for g in range(group):
            turn = lax.rem(g + my_z, group)
            owner = turn * (tiles // per) + t // per

            @pl.when(owner != my_col)
            def _():
                remote(
                    mid_send.at[t, strip(turn), :], mid_recv.at[i, strip(my_col), :],
                    send_m, recv_m.at[i], (my_row, owner),
                ).start()

            @pl.when(owner == my_col)
            def _():
                mid_recv[i, strip(my_col), :] = mid_send[t, strip(turn), :]

    def bias_z(hh):
        def act(step):
            peer = lax.rem(my_z + step, nz)
            mine = bias_recv.at[core, hh, my_row, my_z]
            remote(mine, mine, send_b.at[0, hh], recv_b.at[0, hh], (my_row, 2 * peer + core)).start()

        loop(nz, act)

    def bias_row(hh):
        arrived(bias_recv.at[0, hh, 0, pl.ds(0, nz - 1)], recv_b.at[0, hh])

        def act(step):
            peer = lax.rem(my_row + step, nrow)
            mine = bias_recv.at[core, hh, my_row]
            remote(mine, mine, send_b.at[1, hh], recv_b.at[1, hh], (peer, my_col)).start()

        loop(nrow, act)

    def bias_hand(hh):
        mine = bias_recv.at[core, hh]
        return remote(mine, mine, send_b.at[2, hh], recv_b.at[2, hh], (my_row, my_col + 1 - 2 * core))

    def bias_core(hh):
        arrived(bias_recv.at[0, hh, pl.ds(0, nrow - 1)], recv_b.at[1, hh])
        bias_hand(hh).start()

    for hh in range(halves):
        with scope("waitp"):
            for part in range(parts):
                arrived(prod_recv.at[hh, part, others], recv_p.at[part, hh])
        with scope("unpack"):
            for part in range(parts):
                for d in range(ndev):
                    for c in range(each):
                        at = ((part * each + c) * ndev + d) * high
                        prod_f[at : at + high, :] = prod_recv[hh, part, d, c * high : (c + 1) * high].astype(F32)
        with scope("middle"):
            for tt in range(high):
                t = hh * high + tt
                prods = norm(prod_f[pl.ds(tt, width, stride=high), :], 0)
                prods = jnp.transpose(prods).astype(BF16)
                update = jnp.dot(prods, tri_out_ref[...], preferred_element_type=F32)
                rows = jnp.concatenate([pair_ref[g * tiles + t] for g in range(group)], axis=0)
                middle = rows + tri_gate_s[t] * update
                normed_mid = norm(middle, 1).astype(BF16)
                for g in range(group):
                    out_ref[g * tiles + t] = middle[g * cols_dev : (g + 1) * cols_dev]
                mid_send[t] = normed_mid
                send_rows(t)
                own = lax.dot_general(
                    bias_w_ref[...], normed_mid, (((1,), (1,)), ((), ())), preferred_element_type=F32
                )
                for h in range(heads):
                    bias_f[pl.ds(h * high + tt, 1), :] = own[h : h + 1]
        with scope("bias_z"):
            bias_recv[core, hh, my_row, my_z] = bias_f[...].astype(BF16)
            bias_z(hh)
            if hh > 0:
                bias_row(hh - 1)

    def take(i):
        arrived(mid_recv.at[i, pl.ds(0, (ncol - 1) * cols_dev), :], recv_m.at[i])

    tokens = lax.broadcasted_iota(jnp.int32, (1, total), 1)
    mask = jnp.where(tokens < valid, 0.0, -1000000000.0)
    narrow = lax.broadcasted_iota(jnp.int32, (high, 128), 1) // cols_dev

    def assemble(hh):
        arrived(bias_recv.at[0, hh], recv_b.at[2, hh])
        for h in range(heads):
            for r in range(nrow):
                for half in range(ncol // group):
                    blocks = []
                    for a in range(group):
                        c = half * group + a
                        blocks.append(
                            bias_recv[c % 2, hh, r, c // 2, h * high : (h + 1) * high, :].astype(F32)
                        )
                    for b, piece in enumerate(swap_groups(blocks, narrow, cols_dev)):
                        bias_full[
                            h, pl.ds(r * rows_dev + b * tiles + hh * high, high), pl.ds(half * 128, 128)
                        ] = piece + mask[:, half * 128 : (half + 1) * 128]

    def project(i):
        with scope("take"):
            take(i)
        with scope("project"):
            proj = jnp.dot(mid_recv[i], att_in_ref[...], preferred_element_type=F32)
            qkv_s[i, :, :width] = (proj[:, :width] * head_size ** (-0.5)).astype(BF16)
            qkv_s[i, :, width : 3 * width] = proj[:, width : 3 * width].astype(BF16)
            gate_s[i] = jax.nn.sigmoid(proj[:, 3 * width :])

    ready = per // 2
    for i in range(ready):
        project(i)
    for hh in range(halves - 1):
        with scope("bias_core"):
            bias_core(hh)
    with scope("bias_row"):
        bias_row(halves - 1)
    for hh in range(halves - 1):
        with scope("assemble"):
            assemble(hh)
    with scope("bias_core"):
        bias_core(halves - 1)
    with scope("assemble"):
        assemble(halves - 1)

    block = 128
    head = lax.broadcasted_iota(jnp.int32, (block, width), 1) // head_size

    def home_copy(i, step):
        peer = lax.rem(my_col + step, ncol)
        return remote(
            gated_s.at[i, strip(peer), :], gated_recv.at[i, strip(my_col), :],
            send_g, recv_g.at[i], (my_row, peer),
        )

    def attend(i):
        keys = qkv_s[i, :, width : 2 * width]
        values = jnp.concatenate(
            [qkv_s[i, :, 2 * width : 3 * width], jnp.ones((total, width), BF16)], axis=1
        )
        for first in range(0, total, block):
            query = qkv_s[i, first : first + block, :width]
            top = jnp.zeros((block, width), F32)
            bottom = jnp.ones((block, width), F32)
            for h in range(heads):
                scores = lax.dot_general(
                    jnp.where(head == h, query, jnp.zeros_like(query)), keys,
                    (((1,), (1,)), ((), ())), preferred_element_type=F32,
                )
                scores = scores + bias_full[h, first : first + block, :]
                expo = jnp.exp(scores - jnp.max(scores, axis=1, keepdims=True)).astype(BF16)
                both = jnp.dot(expo, values, preferred_element_type=F32)
                top = jnp.where(head == h, both[:, :width], top)
                bottom = jnp.where(head == h, both[:, width:], bottom)
            gated_s[i, first : first + block, :] = (
                gate_s[i, first : first + block, :] * top / bottom
            ).astype(BF16)
        for step in range(1, ncol):
            home_copy(i, step).start()
        gated_recv[i, strip(my_col), :] = gated_s[i, strip(my_col), :]

    with scope("attend0"):
        lax.fori_loop(0, ready, lambda i, carry: (attend(i), carry)[1], 0)

    def both(i, carry):
        project(i)
        attend(i)
        return carry

    with scope("attend1"):
        lax.fori_loop(ready, per, both, 0)

    def finish(i, carry):
        with scope("waitg"):
            arrived(gated_recv.at[i, pl.ds(0, (ncol - 1) * cols_dev), :], recv_g.at[i])
        added = jnp.dot(gated_recv[i], att_out_ref[...], preferred_element_type=F32)
        for q in range(ncol):
            out_ref[q * per + i] += added[q * cols_dev : (q + 1) * cols_dev]
        return carry

    with scope("finish"):
        lax.fori_loop(0, per, finish, 0)
    with scope("drain"):
        arrived(left_recv.at[others], send_l)
        for part in range(parts):
            arrived(right_recv.at[part, others], send_r.at[part])
            for hh in range(halves):
                arrived(prod_recv.at[hh, part, others], send_p.at[part, hh])
        for i in range(per):
            arrived(mid_recv.at[i, pl.ds(0, (ncol - 1) * cols_dev), :], send_m)
            arrived(mid_recv.at[i, pl.ds(0, (ncol - 1) * cols_dev), :], send_g)
        for hh in range(halves):
            arrived(bias_recv.at[0, hh, 0, pl.ds(0, nz - 1)], send_b.at[0, hh])
            arrived(bias_recv.at[0, hh, pl.ds(0, nrow - 1)], send_b.at[1, hh])
            arrived(bias_recv.at[0, hh], send_b.at[2, hh])


def per_device(pair, valid_length, tri_in, tri_gate, tri_out, att_in, att_bias, att_out):
    rows_dev, cols_dev, width = pair.shape
    heads = att_bias.shape[1]
    nrow, ncol = lax.axis_size("row"), lax.axis_size("col")
    ndev = nrow * ncol
    total = ncol * cols_dev
    tiles = rows_dev // (128 // cols_dev)
    chans = width // ndev
    parts = 2 if chans % 2 == 0 else 1
    each = chans // parts
    per = rows_dev // ncol
    halves = 2 if tiles % 16 == 0 and (tiles // 2) % per == 0 else 1
    high = tiles // halves
    hbm = pl.BlockSpec(memory_space=pltpu.HBM)
    vmem = pl.BlockSpec(memory_space=pltpu.VMEM)
    held = lambda dtype, *shape: pltpu.VMEM(shape, dtype)
    sem = lambda *shape: pltpu.SemaphoreType.DMA(shape) if shape else pltpu.SemaphoreType.DMA
    bias_w = att_bias.T
    args = [pltpu.with_memory_space_constraint(a, pltpu.HBM) for a in (pair, tri_in, tri_gate, tri_out, att_in, bias_w, att_out)]
    return pl.pallas_call(
        functools.partial(kernel, (nrow, ncol, rows_dev, cols_dev, width, heads, parts, halves)),
        out_shape=jax.ShapeDtypeStruct((rows_dev, cols_dev, width), F32),
        in_specs=[pl.BlockSpec(memory_space=pltpu.SMEM)] + [hbm] * 7,
        out_specs=vmem,
        scratch_shapes=[
            *[held(a.dtype, *a.shape) for a in args],
            held(BF16, tiles, 128, width),
            held(F32, 2, width * tiles, 128),
            held(BF16, chans, ndev * tiles, 128),
            held(BF16, chans, ndev * tiles, 128),
            held(BF16, ndev, chans, tiles, 128),
            held(BF16, parts, ndev, each, tiles, 128),
            held(BF16, chans, total, total),
            held(BF16, chans, total, total),
            held(BF16, ndev, halves, chans * high, 128),
            held(BF16, halves, parts, ndev, each * high, 128),
            held(F32, width * high, 128),
            held(F32, tiles, 128, width),
            held(BF16, tiles, 128, width),
            held(BF16, per, total, width),
            held(BF16, per, total, 3 * width),
            held(F32, per, total, width),
            held(F32, heads * high, 128),
            held(BF16, 2, halves, nrow, ncol // 2, heads * high, 128),
            held(F32, heads, total, total),
            held(BF16, per, total, width),
            held(BF16, per, total, width),
            sem(7), sem(), sem(), sem(parts), sem(parts), sem(parts, halves), sem(parts, halves),
            sem(), sem(per), sem(3, halves), sem(3, halves), sem(), sem(per),
        ],
        compiler_params=pltpu.CompilerParams(
            collective_id=0, has_side_effects=True, vmem_limit_bytes=40 * 1024 * 1024
        ),
    )(valid_length, *args)


def solution(mesh):
    placed = (P("row", "col", None), P(), P(), P(), P(), P(), P(), P())
    return jax.shard_map(
        per_device, mesh=mesh, in_specs=placed, out_specs=P("row", "col", None), check_vma=False
    )
```

time: 91.1 us -> 78.7 us (0.86)
  Pallas kernels: 88 us -> 76.9 us
  local copies, waits for them, and re-layouts: 2.26 us -> 0.97 us
    pallas_call x1, Pallas kernels: 88 us -> 76.9 us  [per_device(): pl.pallas_call(functools.partial(kernel, (nrow, ncol, rows_dev, cols_dev,...]
    unnamed x1, local copies, waits for them, and re-layouts: 2.26 us -> 0.97 us
where the time goes in v1:
time: 78.7 us; the launch traced here: 78.5 us
  Pallas kernels  76.9 us (98%)
  local copies, waits for them, and re-layouts  0.97 us (1%)
    pallas_call x1, Pallas kernels, per_device(): pl.pallas_call(functools.partial(kernel, (nrow, ncol, rows_dev, cols_dev,...  76.9 us

profile of v1, /device:TPU:0, one launch (start us, length us, event | category | flops | bytes accessed | tf_op | source)
XLA Modules:
  0.0 78.5 jit_solution(14586585025672835149)
XLA Ops:
  0.7 76.9 %shard_map.82 = f32[64,32,128]{2,1,0:T(8,128)S(1)} custom-call(s32[1]{0:T(128)S(6)} %copy.10.valid_ref, f32[64,32,128]{2,1,0:T(8,128)} %pair_h.1, bf16[128,512]{1,0:T(8,128)(2,1)} %tri_in_h.1, bf16[128,128]{1,0:T(8,128)(2,1)} %tri_gate_h.1, bf16[128,128]{1,0:T(8,128)(2,1)} %tri_out_h.1, bf16[128,512]{1,0:T(8,128)(2,1)} %att_in_h.1, bf16[4,128]{1,0:T(4,128)(2,1)} %bitcast.1, ...), custom_call_target="tpu_custom_call" | custom-call | tf_op jit(solution)/shard_map/pallas_call | solution.py:432
  77.5 1.0 %copy.11 = f32[64,32,128]{2,1,0:T(8,128)} copy(f32[64,32,128]{2,1,0:T(8,128)S(1)} %shard_map.82) | data formatting | bytes 2097152

commit v2 on v1

--- a/solution.py
+++ b/solution.py
@@ -42,7 +42,7 @@
     out_ref,
     pair_ref, tri_in_ref, tri_gate_ref, tri_out_ref, att_in_ref, bias_w_ref, att_out_ref,
     normed_s, edge_f, left_send, right_send, left_recv, right_recv, left_s, right_s,
-    prod_send, prod_recv, prod_f, tri_gate_s, mid_send, mid_recv, qkv_s, gate_s,
+    prod_send, prod_recv, prod_f, tri_gate_s, pair_s, middle_s, tri_out_s, mid_send, mid_recv, qkv_s, gate_s,
     bias_f, bias_recv, bias_full, gated_s, gated_recv,
     sem_in, send_l, recv_l, send_r, recv_r, send_p, recv_p, send_m, recv_m,
     send_b, recv_b, send_g, recv_g,
@@ -96,22 +96,30 @@
     lane_col = my_col * cols_dev + lanes % cols_dev
     lane_row = my_row * rows_dev + (lanes // cols_dev) * tiles
 
-    def edges(side):
+    def edge(side, t):
         first = 2 * side * width
+        if side == 0:
+            rows = jnp.concatenate([pair_ref[g * tiles + t] for g in range(group)], axis=0)
+            normed_s[t] = norm(rows, 1).astype(BF16)
+        proj = jnp.dot(
+            normed_s[t], tri_in_ref[:, first : first + 2 * width], preferred_element_type=F32
+        )
+        keep = jnp.where((lane_row + t < valid) & (lane_col < valid), 1.0, 0.0)
+        return jnp.transpose(jax.nn.sigmoid(proj[:, :width]) * proj[:, width:]) * keep
+
+    def left_edges(hh):
+        for tt in range(high):
+            edge_f[0, pl.ds(hh * width * high + tt, width, stride=high), :] = edge(0, hh * high + tt)
+        for d in range(ndev):
+            for c in range(chans):
+                at = hh * width * high + (c * ndev + d) * high
+                left_send[hh, d, c * high : (c + 1) * high] = edge_f[0, at : at + high, :].astype(BF16)
+
+    def right_edges():
         for t in range(tiles):
-            if side == 0:
-                rows = jnp.concatenate([pair_ref[g * tiles + t] for g in range(group)], axis=0)
-                normed_s[t] = norm(rows, 1).astype(BF16)
-            proj = jnp.dot(
-                normed_s[t], tri_in_ref[:, first : first + 2 * width], preferred_element_type=F32
-            )
-            keep = jnp.where((lane_row + t < valid) & (lane_col < valid), 1.0, 0.0)
-            edge = jax.nn.sigmoid(proj[:, :width]) * proj[:, width:]
-            edge_f[side, pl.ds(t, width, stride=tiles), :] = jnp.transpose(edge) * keep
-
-    def pack(side, target):
+            edge_f[1, pl.ds(t, width, stride=tiles), :] = edge(1, t)
         for c in range(chans):
-            target[c] = edge_f[side, pl.ds(c * ndev * tiles, ndev * tiles), :].astype(BF16)
+            right_send[c] = edge_f[1, pl.ds(c * ndev * tiles, ndev * tiles), :].astype(BF16)
 
     def share(peer):
         return pl.ds(pl.multiple_of(peer * tiles, tiles), tiles)
@@ -121,9 +129,9 @@
             src_ref=src, dst_ref=dst, send_sem=send, recv_sem=recv, device_id=where, device_id_type=MESH
         )
 
-    def left_copy(step):
+    def left_copy(hh, step):
         peer, where = other(step)
-        return remote(left_send.at[:, share(peer), :], left_recv.at[me], send_l, recv_l, where)
+        return remote(left_send.at[hh, peer], left_recv.at[hh, me], send_l.at[hh], recv_l.at[hh], where)
 
     def right_copy(part, step):
         peer, where = other(step)
@@ -133,39 +141,44 @@
             send_r.at[part], recv_r.at[part], where,
         )
 
-    with scope("edges0"):
-        edges(0)
-        pack(0, left_send)
-    with scope("barrier"):
-        pl.semaphore_wait(barrier, ndev - 1)
-    with scope("sendl"):
-        loop(ndev, lambda step: left_copy(step).start())
+    for hh in range(halves):
+        with scope("edges0"):
+            left_edges(hh)
+        if hh == 0:
+            with scope("barrier"):
+                pl.semaphore_wait(barrier, ndev - 1)
+        with scope("sendl"):
+            loop(ndev, lambda step: left_copy(hh, step).start())
+            left_recv[hh, me] = left_send[hh, me]
     with scope("edges1"):
-        edges(1)
-        pack(1, right_send)
+        right_edges()
     with scope("sendr"):
         for part in range(parts):
             loop(ndev, lambda step: right_copy(part, step).start())
+            right_recv[part, me] = right_send[part * each : (part + 1) * each, share(me), :]
     with scope("gate"):
-        left_recv[me] = left_send[:, share(me), :]
-        for part in range(parts):
-            right_recv[part, me] = right_send[part * each : (part + 1) * each, share(me), :]
         for k in (2, 3, 5, 4, 6):
             loads[k].wait()
+        tri_out_s[...] = jnp.transpose(tri_out_ref[...].astype(F32)).astype(BF16)
         for t in range(tiles):
             tri_gate_s[t] = jax.nn.sigmoid(
-                jnp.dot(normed_s[t], tri_gate_ref[...], preferred_element_type=F32)
+                lax.dot_general(
+                    tri_gate_ref[...], normed_s[t], (((0,), (1,)), ((), ())), preferred_element_type=F32
+                )
             )
+            rows = jnp.concatenate([pair_ref[g * tiles + t] for g in range(group)], axis=0)
+            pair_s[t] = jnp.transpose(rows)
     others = pl.ds(0, ndev - 1)
     with scope("waitl"):
-        arrived(left_recv.at[others], recv_l)
+        for hh in range(halves):
+            arrived(left_recv.at[hh, others], recv_l.at[hh])
 
     lane = lax.broadcasted_iota(jnp.int32, (tiles, 128), 1) // cols_dev
 
     def spread(load, operand):
         for r in range(nrow):
             for half in range(ncol // group):
-                blocks = [load(r * ncol + half * group + a).astype(F32) for a in range(group)]
+                blocks = [load(r * ncol + half * group + a) for a in range(group)]
                 for b, piece in enumerate(swap_groups(blocks, lane, cols_dev)):
                     operand[
                         pl.ds(r * rows_dev + b * tiles, tiles), pl.ds(half * 128, 128)
@@ -181,13 +194,18 @@
 
     with scope("spreadl"):
         for c in range(chans):
-            spread(lambda d: left_recv[d, c], left_s.at[c])
+            spread(
+                lambda d: jnp.concatenate(
+                    [left_recv[hh, d, c * high : (c + 1) * high].astype(F32) for hh in range(halves)], axis=0
+                ),
+                left_s.at[c],
+            )
     for part in range(parts):
         with scope("waitr"):
             arrived(right_recv.at[part, others], recv_r.at[part])
         with scope("products"):
             for c in range(part * each, (part + 1) * each):
-                spread(lambda d: right_recv[part, d, c - part * each], right_s.at[c])
+                spread(lambda d: right_recv[part, d, c - part * each].astype(F32), right_s.at[c])
                 products = lax.dot_general(
                     left_s[c], right_s[c], (((1,), (1,)), ((), ())), preferred_element_type=F32
                 )
@@ -269,26 +287,25 @@
         with scope("middle"):
             for tt in range(high):
                 t = hh * high + tt
-                prods = norm(prod_f[pl.ds(tt, width, stride=high), :], 0)
-                prods = jnp.transpose(prods).astype(BF16)
-                update = jnp.dot(prods, tri_out_ref[...], preferred_element_type=F32)
-                rows = jnp.concatenate([pair_ref[g * tiles + t] for g in range(group)], axis=0)
-                middle = rows + tri_gate_s[t] * update
-                normed_mid = norm(middle, 1).astype(BF16)
-                for g in range(group):
-                    out_ref[g * tiles + t] = middle[g * cols_dev : (g + 1) * cols_dev]
-                mid_send[t] = normed_mid
-                send_rows(t)
-                own = lax.dot_general(
-                    bias_w_ref[...], normed_mid, (((1,), (1,)), ((), ())), preferred_element_type=F32
-                )
+                prods = norm(prod_f[pl.ds(tt, width, stride=high), :], 0).astype(BF16)
+                update = jnp.dot(tri_out_s[...], prods, preferred_element_type=F32)
+                middle = pair_s[t] + tri_gate_s[t] * update
+                middle_s[t] = middle
+                normed_mid = norm(middle, 0)
+                own = jnp.dot(bias_w_ref[...], normed_mid.astype(BF16), preferred_element_type=F32)
                 for h in range(heads):
                     bias_f[pl.ds(h * high + tt, 1), :] = own[h : h + 1]
+                mid_send[t] = jnp.transpose(normed_mid).astype(BF16)
         with scope("bias_z"):
             bias_recv[core, hh, my_row, my_z] = bias_f[...].astype(BF16)
             bias_z(hh)
+        with scope("send_rows"):
+            early = range(high // 2) if hh == 0 and halves > 1 else range(high)
             if hh > 0:
-                bias_row(hh - 1)
+                for tt in range(high // 2 if hh == 1 else high, high):
+                    send_rows((hh - 1) * high + tt)
+            for tt in early:
+                send_rows(hh * high + tt)
 
     def take(i):
         arrived(mid_recv.at[i, pl.ds(0, (ncol - 1) * cols_dev), :], recv_m.at[i])
@@ -322,21 +339,23 @@
             qkv_s[i, :, width : 3 * width] = proj[:, width : 3 * width].astype(BF16)
             gate_s[i] = jax.nn.sigmoid(proj[:, 3 * width :])
 
+    with scope("keep_middle"):
+        for t in range(tiles):
+            middle = jnp.transpose(middle_s[t])
+            for g in range(group):
+                out_ref[g * tiles + t] = middle[g * cols_dev : (g + 1) * cols_dev]
+    for hh in range(halves):
+        with scope("bias_row"):
+            bias_row(hh)
+    for hh in range(halves):
+        with scope("bias_core"):
+            bias_core(hh)
     ready = per // 2
     for i in range(ready):
         project(i)
-    for hh in range(halves - 1):
-        with scope("bias_core"):
-            bias_core(hh)
-    with scope("bias_row"):
-        bias_row(halves - 1)
-    for hh in range(halves - 1):
+    for hh in range(halves):
         with scope("assemble"):
             assemble(hh)
-    with scope("bias_core"):
-        bias_core(halves - 1)
-    with scope("assemble"):
-        assemble(halves - 1)
 
     block = 128
     head = lax.broadcasted_iota(jnp.int32, (block, width), 1) // head_size
@@ -396,7 +415,8 @@
     with scope("finish"):
         lax.fori_loop(0, per, finish, 0)
     with scope("drain"):
-        arrived(left_recv.at[others], send_l)
+        for hh in range(halves):
+            arrived(left_recv.at[hh, others], send_l.at[hh])
         for part in range(parts):
             arrived(right_recv.at[part, others], send_r.at[part])
             for hh in range(halves):
@@ -438,16 +458,19 @@
             *[held(a.dtype, *a.shape) for a in args],
             held(BF16, tiles, 128, width),
             held(F32, 2, width * tiles, 128),
+            held(BF16, halves, ndev, chans * high, 128),
             held(BF16, chans, ndev * tiles, 128),
-            held(BF16, chans, ndev * tiles, 128),
-            held(BF16, ndev, chans, tiles, 128),
+            held(BF16, halves, ndev, chans * high, 128),
             held(BF16, parts, ndev, each, tiles, 128),
             held(BF16, chans, total, total),
             held(BF16, chans, total, total),
             held(BF16, ndev, halves, chans * high, 128),
             held(BF16, halves, parts, ndev, each * high, 128),
             held(F32, width * high, 128),
-            held(F32, tiles, 128, width),
+            held(F32, tiles, width, 128),
+            held(F32, tiles, width, 128),
+            held(F32, tiles, width, 128),
+            held(BF16, width, width),
             held(BF16, tiles, 128, width),
             held(BF16, per, total, width),
             held(BF16, per, total, 3 * width),
@@ -457,7 +480,7 @@
             held(F32, heads, total, total),
             held(BF16, per, total, width),
             held(BF16, per, total, width),
-            sem(7), sem(), sem(), sem(parts), sem(parts), sem(parts, halves), sem(parts, halves),
+            sem(7), sem(halves), sem(halves), sem(parts), sem(parts), sem(parts, halves), sem(parts, halves),
             sem(), sem(per), sem(3, halves), sem(3, halves), sem(), sem(per),
         ],
         compiler_params=pltpu.CompilerParams(

time: 78.7 us -> 73 us (0.928)
  Pallas kernels: 76.9 us -> 71.2 us
    pallas_call x1, Pallas kernels: 76.9 us -> 71.2 us  [per_device(): pl.pallas_call(functools.partial(kernel, (nrow, ncol, rows_dev, cols_dev,...]
where the time goes in v2:
time: 73 us; the launch traced here: 72.9 us
  Pallas kernels  71.2 us (98%)
  local copies, waits for them, and re-layouts  0.97 us (1%)
    pallas_call x1, Pallas kernels, per_device(): pl.pallas_call(functools.partial(kernel, (nrow, ncol, rows_dev, cols_dev,...  71.2 us

profile of v2, /device:TPU:0, one launch (start us, length us, event | category | flops | bytes accessed | tf_op | source)
XLA Modules:
  0.0 72.9 jit_solution(3118446426673955277)
XLA Ops:
  0.7 71.2 %shard_map.82 = f32[64,32,128]{2,1,0:T(8,128)S(1)} custom-call(s32[1]{0:T(128)S(6)} %copy.10.valid_ref, f32[64,32,128]{2,1,0:T(8,128)} %pair_h.1, bf16[128,512]{1,0:T(8,128)(2,1)} %tri_in_h.1, bf16[128,128]{1,0:T(8,128)(2,1)} %tri_gate_h.1, bf16[128,128]{1,0:T(8,128)(2,1)} %tri_out_h.1, bf16[128,512]{1,0:T(8,128)(2,1)} %att_in_h.1, bf16[4,128]{1,0:T(4,128)(2,1)} %bitcast.1, ...), custom_call_target="tpu_custom_call" | custom-call | tf_op jit(solution)/shard_map/pallas_call | solution.py:452
  71.9 1.0 %copy.11 = f32[64,32,128]{2,1,0:T(8,128)} copy(f32[64,32,128]{2,1,0:T(8,128)S(1)} %shard_map.82) | data formatting | bytes 2097152

commit v3 on v2

--- a/solution.py
+++ b/solution.py
@@ -42,10 +42,10 @@
     out_ref,
     pair_ref, tri_in_ref, tri_gate_ref, tri_out_ref, att_in_ref, bias_w_ref, att_out_ref,
     normed_s, edge_f, left_send, right_send, left_recv, right_recv, left_s, right_s,
-    prod_send, prod_recv, prod_f, tri_gate_s, pair_s, middle_s, tri_out_s, mid_send, mid_recv, qkv_s, gate_s,
+    prod_send, prod_recv, prod_f, tri_gate_s, pair_s, middle_s, tri_out_s, mid_send, mid_recv, kv_s, query_s, gate_s,
     bias_f, bias_recv, bias_full, gated_s, gated_recv,
     sem_in, send_l, recv_l, send_r, recv_r, send_p, recv_p, send_m, recv_m,
-    send_b, recv_b, send_g, recv_g,
+    send_b, recv_z, recv_b, send_g, recv_g,
 ):
     nrow, ncol, rows_dev, cols_dev, width, heads, parts, halves = dims
     ndev = nrow * ncol
@@ -55,6 +55,7 @@
     chans = width // ndev
     each = chans // parts
     per = rows_dev // ncol
+    span = tiles // per
     high = tiles // halves
     nz = ncol // 2
     head_size = width // heads
@@ -81,12 +82,9 @@
 
     with scope("signal"):
         barrier = pltpu.get_barrier_semaphore()
-        loop(
-            ndev,
-            lambda step: pl.semaphore_signal(
-                barrier, inc=1, device_id=other(step)[1], device_id_type=MESH
-            ),
-        )
+        for r in range(nrow):
+            for c in range(ncol):
+                pl.semaphore_signal(barrier, inc=1, device_id=(r, c), device_id_type=MESH)
     with scope("inputs"):
         for k in (0, 1):
             loads[k].wait()
@@ -146,7 +144,7 @@
             left_edges(hh)
         if hh == 0:
             with scope("barrier"):
-                pl.semaphore_wait(barrier, ndev - 1)
+                pl.semaphore_wait(barrier, ndev)
         with scope("sendl"):
             loop(ndev, lambda step: left_copy(hh, step).start())
             left_recv[hh, me] = left_send[hh, me]
@@ -224,18 +222,19 @@
                                     hh * high : (hh + 1) * high
                                 ].astype(BF16)
         with scope("sendp"):
-            for hh in range(halves):
-                loop(ndev, lambda step: prod_copy(part, hh, step).start())
-                prod_recv[hh, part, me] = prod_send[me, hh, part * each * high : (part + 1) * each * high]
+            for hh in range(halves if part == parts - 1 else 1):
+                for p in range(part if hh == 0 else 0, part + 1):
+                    loop(ndev, lambda step: prod_copy(p, hh, step).start())
+                    prod_recv[hh, p, me] = prod_send[me, hh, p * each * high : (p + 1) * each * high]
 
     def strip(peer):
         return pl.ds(pl.multiple_of(peer * cols_dev, cols_dev), cols_dev)
 
     def send_rows(t):
-        i = t % per
+        i = t // span
         for g in range(group):
             turn = lax.rem(g + my_z, group)
-            owner = turn * (tiles // per) + t // per
+            owner = turn * span + t % span
 
             @pl.when(owner != my_col)
             def _():
@@ -248,23 +247,25 @@
             def _():
                 mid_recv[i, strip(my_col), :] = mid_send[t, strip(turn), :]
 
+    def bias_block(hh, z):
+        block = bias_recv.at[core, hh, my_row, z]
+        for step in range(1, nrow):
+            peer = lax.rem(my_row + step, nrow)
+            remote(block, block, send_b.at[1, hh], recv_b.at[1, hh], (peer, my_col)).start()
+
     def bias_z(hh):
-        def act(step):
+        mine = bias_recv.at[core, hh, my_row, my_z]
+        for step in range(1, nz):
             peer = lax.rem(my_z + step, nz)
-            mine = bias_recv.at[core, hh, my_row, my_z]
-            remote(mine, mine, send_b.at[0, hh], recv_b.at[0, hh], (my_row, 2 * peer + core)).start()
-
-        loop(nz, act)
+            remote(mine, mine, send_b.at[0, hh], recv_z.at[hh, my_z], (my_row, 2 * peer + core)).start()
+        bias_block(hh, my_z)
 
     def bias_row(hh):
-        arrived(bias_recv.at[0, hh, 0, pl.ds(0, nz - 1)], recv_b.at[0, hh])
-
-        def act(step):
-            peer = lax.rem(my_row + step, nrow)
-            mine = bias_recv.at[core, hh, my_row]
-            remote(mine, mine, send_b.at[1, hh], recv_b.at[1, hh], (peer, my_col)).start()
-
-        loop(nrow, act)
+        turn = 1 - 2 * (my_z // (nz // 2))
+        for step in range(1, nz):
+            z = lax.rem(my_z + turn * step + nz, nz)
+            arrived(bias_recv.at[0, hh, 0, 0], recv_z.at[hh, z])
+            bias_block(hh, z)
 
     def bias_hand(hh):
         mine = bias_recv.at[core, hh]
@@ -300,9 +301,9 @@
             bias_recv[core, hh, my_row, my_z] = bias_f[...].astype(BF16)
             bias_z(hh)
         with scope("send_rows"):
-            early = range(high // 2) if hh == 0 and halves > 1 else range(high)
+            early = range(3 * high // 4) if hh == 0 and halves > 1 else range(high)
             if hh > 0:
-                for tt in range(high // 2 if hh == 1 else high, high):
+                for tt in range(3 * high // 4 if hh == 1 else high, high):
                     send_rows((hh - 1) * high + tt)
             for tt in early:
                 send_rows(hh * high + tt)
@@ -327,7 +328,7 @@
                         )
                     for b, piece in enumerate(swap_groups(blocks, narrow, cols_dev)):
                         bias_full[
-                            h, pl.ds(r * rows_dev + b * tiles + hh * high, high), pl.ds(half * 128, 128)
+                            hh, h, pl.ds((r * group + b) * high, high), pl.ds(half * 128, 128)
                         ] = piece + mask[:, half * 128 : (half + 1) * 128]
 
     def project(i):
@@ -335,45 +336,45 @@
             take(i)
         with scope("project"):
             proj = jnp.dot(mid_recv[i], att_in_ref[...], preferred_element_type=F32)
-            qkv_s[i, :, :width] = (proj[:, :width] * head_size ** (-0.5)).astype(BF16)
-            qkv_s[i, :, width : 3 * width] = proj[:, width : 3 * width].astype(BF16)
-            gate_s[i] = jax.nn.sigmoid(proj[:, 3 * width :])
-
+            kv_s[i] = proj[:, width : 3 * width].astype(BF16)
+            query = proj[:, :width] * head_size ** (-0.5)
+            gate = jax.nn.sigmoid(proj[:, 3 * width :])
+            for hh in range(halves):
+                pick = lambda x: jnp.concatenate(
+                    [x[at : at + high] for at in range(hh * high, total, tiles)], axis=0
+                )
+                query_s[i, hh] = pick(query).astype(BF16)
+                gate_s[i, hh] = pick(gate)
+
+    with scope("bias_row"):
+        bias_row(0)
     with scope("keep_middle"):
         for t in range(tiles):
             middle = jnp.transpose(middle_s[t])
             for g in range(group):
                 out_ref[g * tiles + t] = middle[g * cols_dev : (g + 1) * cols_dev]
-    for hh in range(halves):
-        with scope("bias_row"):
-            bias_row(hh)
-    for hh in range(halves):
-        with scope("bias_core"):
-            bias_core(hh)
-    ready = per // 2
-    for i in range(ready):
-        project(i)
-    for hh in range(halves):
-        with scope("assemble"):
-            assemble(hh)
-
-    block = 128
+    with scope("bias_core"):
+        bias_core(0)
+
+    block = min(128, total // halves)
+    own_cols = cols_dev // halves
     head = lax.broadcasted_iota(jnp.int32, (block, width), 1) // head_size
 
-    def home_copy(i, step):
+    def share_cols(peer):
+        return pl.ds(pl.multiple_of(peer * own_cols, own_cols), own_cols)
+
+    def home_copy(hh, i, step):
         peer = lax.rem(my_col + step, ncol)
         return remote(
-            gated_s.at[i, strip(peer), :], gated_recv.at[i, strip(my_col), :],
-            send_g, recv_g.at[i], (my_row, peer),
+            gated_s.at[hh, i, share_cols(peer), :], gated_recv.at[hh, i, share_cols(my_col), :],
+            send_g, recv_g.at[hh, i], (my_row, peer),
         )
 
-    def attend(i):
-        keys = qkv_s[i, :, width : 2 * width]
-        values = jnp.concatenate(
-            [qkv_s[i, :, 2 * width : 3 * width], jnp.ones((total, width), BF16)], axis=1
-        )
-        for first in range(0, total, block):
-            query = qkv_s[i, first : first + block, :width]
+    def attend(hh, i):
+        keys = kv_s[i, :, :width]
+        values = jnp.concatenate([kv_s[i, :, width:], jnp.ones((total, width), BF16)], axis=1)
+        for first in range(0, total // halves, block):
+            query = query_s[i, hh, first : first + block, :]
             top = jnp.zeros((block, width), F32)
             bottom = jnp.ones((block, width), F32)
             for h in range(heads):
@@ -381,39 +382,63 @@
                     jnp.where(head == h, query, jnp.zeros_like(query)), keys,
                     (((1,), (1,)), ((), ())), preferred_element_type=F32,
                 )
-                scores = scores + bias_full[h, first : first + block, :]
+                scores = scores + bias_full[hh, h, first : first + block, :]
                 expo = jnp.exp(scores - jnp.max(scores, axis=1, keepdims=True)).astype(BF16)
                 both = jnp.dot(expo, values, preferred_element_type=F32)
                 top = jnp.where(head == h, both[:, :width], top)
                 bottom = jnp.where(head == h, both[:, width:], bottom)
-            gated_s[i, first : first + block, :] = (
-                gate_s[i, first : first + block, :] * top / bottom
+            gated_s[hh, i, first : first + block, :] = (
+                gate_s[i, hh, first : first + block, :] * top / bottom
             ).astype(BF16)
         for step in range(1, ncol):
-            home_copy(i, step).start()
-        gated_recv[i, strip(my_col), :] = gated_s[i, strip(my_col), :]
-
-    with scope("attend0"):
-        lax.fori_loop(0, ready, lambda i, carry: (attend(i), carry)[1], 0)
-
-    def both(i, carry):
+            home_copy(hh, i, step).start()
+        gated_recv[hh, i, share_cols(my_col), :] = gated_s[hh, i, share_cols(my_col), :]
+
+    def run(first, last, act):
+        def body(i, carry):
+            act(i)
+            return carry
+
+        lax.fori_loop(first, last, body, 0)
+
+    def first_pass(i):
         project(i)
-        attend(i)
-        return carry
-
-    with scope("attend1"):
-        lax.fori_loop(ready, per, both, 0)
-
-    def finish(i, carry):
+        attend(0, i)
+
+    ready = per // halves
+    project(0)
+    with scope("bias_row"):
+        for hh in range(1, halves):
+            bias_row(hh)
+    with scope("assemble"):
+        assemble(0)
+    with scope("attend"):
+        attend(0, 0)
+        run(1, ready, first_pass)
+    with scope("bias_core"):
+        for hh in range(1, halves):
+            bias_core(hh)
+    with scope("attend"):
+        run(ready, per, first_pass)
+    for hh in range(1, halves):
+        with scope("assemble"):
+            assemble(hh)
+        with scope("attend"):
+            run(0, per, lambda i: attend(hh, i))
+
+    def finish(hh, i):
         with scope("waitg"):
-            arrived(gated_recv.at[i, pl.ds(0, (ncol - 1) * cols_dev), :], recv_g.at[i])
-        added = jnp.dot(gated_recv[i], att_out_ref[...], preferred_element_type=F32)
+            arrived(gated_recv.at[hh, i, pl.ds(0, (ncol - 1) * own_cols), :], recv_g.at[hh, i])
+        added = jnp.dot(gated_recv[hh, i], att_out_ref[...], preferred_element_type=F32)
         for q in range(ncol):
-            out_ref[q * per + i] += added[q * cols_dev : (q + 1) * cols_dev]
-        return carry
+            row = (q // span) * tiles + i * span + q % span
+            for m in range(own_cols // high):
+                at = q * own_cols + m * high
+                out_ref[row, m * tiles + hh * high : m * tiles + (hh + 1) * high] += added[at : at + high]
 
     with scope("finish"):
-        lax.fori_loop(0, per, finish, 0)
+        for hh in range(halves):
+            run(0, per, lambda i: finish(hh, i))
     with scope("drain"):
         for hh in range(halves):
             arrived(left_recv.at[hh, others], send_l.at[hh])
@@ -473,15 +498,16 @@
             held(BF16, width, width),
             held(BF16, tiles, 128, width),
             held(BF16, per, total, width),
-            held(BF16, per, total, 3 * width),
-            held(F32, per, total, width),
+            held(BF16, per, total, 2 * width),
+            held(BF16, per, halves, total // halves, width),
+            held(F32, per, halves, total // halves, width),
             held(F32, heads * high, 128),
             held(BF16, 2, halves, nrow, ncol // 2, heads * high, 128),
-            held(F32, heads, total, total),
-            held(BF16, per, total, width),
-            held(BF16, per, total, width),
+            held(F32, halves, heads, total // halves, total),
+            held(BF16, halves, per, total // halves, width),
+            held(BF16, halves, per, total // halves, width),
             sem(7), sem(halves), sem(halves), sem(parts), sem(parts), sem(parts, halves), sem(parts, halves),
-            sem(), sem(per), sem(3, halves), sem(3, halves), sem(), sem(per),
+            sem(), sem(per), sem(3, halves), sem(halves, ncol // 2), sem(3, halves), sem(), sem(halves, per),
         ],
         compiler_params=pltpu.CompilerParams(
             collective_id=0, has_side_effects=True, vmem_limit_bytes=40 * 1024 * 1024

time: 73 us -> 69.3 us (0.949)
  Pallas kernels: 71.2 us -> 67.5 us
    pallas_call x1, Pallas kernels: 71.2 us -> 67.5 us  [per_device(): pl.pallas_call(functools.partial(kernel, (nrow, ncol, rows_dev, cols_dev,...]
where the time goes in v3:
time: 69.3 us; the launch traced here: 69.1 us
  Pallas kernels  67.5 us (97%)
  local copies, waits for them, and re-layouts  0.97 us (1%)
    pallas_call x1, Pallas kernels, per_device(): pl.pallas_call(functools.partial(kernel, (nrow, ncol, rows_dev, cols_dev,...  67.5 us

profile of v3, /device:TPU:0, one launch (start us, length us, event | category | flops | bytes accessed | tf_op | source)
XLA Modules:
  0.0 69.1 jit_solution(7264887896706437147)
XLA Ops:
  0.7 67.5 %shard_map.82 = f32[64,32,128]{2,1,0:T(8,128)S(1)} custom-call(s32[1]{0:T(128)S(6)} %copy.10.valid_ref, f32[64,32,128]{2,1,0:T(8,128)} %pair_h.1, bf16[128,512]{1,0:T(8,128)(2,1)} %tri_in_h.1, bf16[128,128]{1,0:T(8,128)(2,1)} %tri_gate_h.1, bf16[128,128]{1,0:T(8,128)(2,1)} %tri_out_h.1, bf16[128,512]{1,0:T(8,128)(2,1)} %att_in_h.1, bf16[4,128]{1,0:T(4,128)(2,1)} %bitcast.1, ...), custom_call_target="tpu_custom_call" | custom-call | tf_op jit(solution)/shard_map/pallas_call | solution.py:477
  68.2 1.0 %copy.11 = f32[64,32,128]{2,1,0:T(8,128)} copy(f32[64,32,128]{2,1,0:T(8,128)S(1)} %shard_map.82) | data formatting | bytes 2097152

commit v4 on v3

--- a/solution.py
+++ b/solution.py
@@ -41,19 +41,22 @@
     valid_ref, pair_h, tri_in_h, tri_gate_h, tri_out_h, att_in_h, bias_w_h, att_out_h,
     out_ref,
     pair_ref, tri_in_ref, tri_gate_ref, tri_out_ref, att_in_ref, bias_w_ref, att_out_ref,
-    normed_s, edge_f, left_send, right_send, left_recv, right_recv, left_s, right_s,
-    prod_send, prod_recv, prod_f, tri_gate_s, pair_s, middle_s, tri_out_s, mid_send, mid_recv, kv_s, query_s, gate_s,
+    tri_in_s, tri_gate_t, tri_out_s, normed_s, pair_s, middle_s, gate_t, edge_f,
+    near_send, near_recv, far_send, far_recv, near_left, near_right, far_left, far_right,
+    near_psend, near_precv, far_psend, far_precv, prod_f,
+    mid_send, mid_recv, kv_s, query_s, gate_s,
     bias_f, bias_recv, bias_full, gated_s, gated_recv,
-    sem_in, send_l, recv_l, send_r, recv_r, send_p, recv_p, send_m, recv_m,
+    sem_in, sem_pair, send_n, recv_n, send_f, recv_f, send_pn, recv_pn, send_pf, recv_pf, send_m, recv_m,
     send_b, recv_z, recv_b, send_g, recv_g,
 ):
-    nrow, ncol, rows_dev, cols_dev, width, heads, parts, halves = dims
+    nrow, ncol, rows_dev, cols_dev, width, heads, far, near, parts, halves = dims
     ndev = nrow * ncol
     total = ncol * cols_dev
     group = 128 // cols_dev
     tiles = rows_dev // group
-    chans = width // ndev
-    each = chans // parts
+    each = near // parts if parts else 0
+    side_cols = ncol // 2
+    team = nrow * side_cols
     per = rows_dev // ncol
     span = tiles // per
     high = tiles // halves
@@ -62,11 +65,17 @@
     my_row, my_col = lax.axis_index("row"), lax.axis_index("col")
     me = my_row * ncol + my_col
     core, my_z = lax.rem(my_col, 2), my_col // 2
-
-    held = (pair_ref, tri_in_ref, tri_gate_ref, tri_out_ref, att_in_ref, bias_w_ref, att_out_ref)
-    given = (pair_h, tri_in_h, tri_gate_h, tri_out_h, att_in_h, bias_w_h, att_out_h)
+    my_side, my_rank = my_col // side_cols, my_row * side_cols + lax.rem(my_col, side_cols)
+
+    held = (tri_in_ref, tri_gate_ref, tri_out_ref, att_in_ref, bias_w_ref, att_out_ref)
+    given = (tri_in_h, tri_gate_h, tri_out_h, att_in_h, bias_w_h, att_out_h)
     loads = [pltpu.make_async_copy(g, v, sem_in.at[k]) for k, (g, v) in enumerate(zip(given, held))]
-    for k in (0, 1, 2, 3, 5, 4, 6):
+    loads[0].start()
+    for hh in range(halves):
+        for g in range(group):
+            some = pl.ds(g * tiles + hh * high, high)
+            pltpu.make_async_copy(pair_h.at[some], pair_ref.at[some], sem_pair.at[hh]).start()
+    for k in (1, 2, 4, 3, 5):
         loads[k].start()
 
     def other(step):
@@ -86,146 +95,192 @@
             for c in range(ncol):
                 pl.semaphore_signal(barrier, inc=1, device_id=(r, c), device_id_type=MESH)
     with scope("inputs"):
-        for k in (0, 1):
-            loads[k].wait()
+        loads[0].wait()
+        tri_in_s[...] = jnp.transpose(tri_in_ref[...].astype(F32)).astype(BF16)
     valid = valid_ref[0]
 
     lanes = lax.broadcasted_iota(jnp.int32, (1, 128), 1)
     lane_col = my_col * cols_dev + lanes % cols_dev
     lane_row = my_row * rows_dev + (lanes // cols_dev) * tiles
 
-    def edge(side, t):
-        first = 2 * side * width
-        if side == 0:
+    def edges(hh):
+        arrived(pair_ref.at[pl.ds(0, group * high)], sem_pair.at[hh])
+        for tt in range(high):
+            t = hh * high + tt
             rows = jnp.concatenate([pair_ref[g * tiles + t] for g in range(group)], axis=0)
-            normed_s[t] = norm(rows, 1).astype(BF16)
-        proj = jnp.dot(
-            normed_s[t], tri_in_ref[:, first : first + 2 * width], preferred_element_type=F32
-        )
-        keep = jnp.where((lane_row + t < valid) & (lane_col < valid), 1.0, 0.0)
-        return jnp.transpose(jax.nn.sigmoid(proj[:, :width]) * proj[:, width:]) * keep
-
-    def left_edges(hh):
-        for tt in range(high):
-            edge_f[0, pl.ds(hh * width * high + tt, width, stride=high), :] = edge(0, hh * high + tt)
+            rows = jnp.transpose(rows)
+            pair_s[t] = rows
+            normed = norm(rows, 0).astype(BF16)
+            normed_s[t] = normed
+            keep = jnp.where((lane_row + t < valid) & (lane_col < valid), 1.0, 0.0)
+            for side in range(2):
+                proj = jnp.dot(
+                    tri_in_s[2 * side * width : 2 * (side + 1) * width, :], normed, preferred_element_type=F32
+                )
+                edge_f[side, hh, pl.ds(tt, width, stride=high), :] = (
+                    jax.nn.sigmoid(proj[:width]) * proj[width:] * keep
+                )
+
+    def near_channel(k, rank):
+        return far * ndev + k * team + rank
+
+    def near_pack(part, hh):
+        for rank in range(team):
+            for side in range(2):
+                for k in range(each):
+                    at = near_channel(part * each + k, rank) * high
+                    near_send[part, hh, rank, side, k * high : (k + 1) * high] = edge_f[
+                        side, hh, at : at + high, :
+                    ].astype(BF16)
+
+    def far_pack():
         for d in range(ndev):
-            for c in range(chans):
-                at = hh * width * high + (c * ndev + d) * high
-                left_send[hh, d, c * high : (c + 1) * high] = edge_f[0, at : at + high, :].astype(BF16)
-
-    def right_edges():
-        for t in range(tiles):
-            edge_f[1, pl.ds(t, width, stride=tiles), :] = edge(1, t)
-        for c in range(chans):
-            right_send[c] = edge_f[1, pl.ds(c * ndev * tiles, ndev * tiles), :].astype(BF16)
-
-    def share(peer):
-        return pl.ds(pl.multiple_of(peer * tiles, tiles), tiles)
+            for side in range(2):
+                for f in range(far):
+                    for hh in range(halves):
+                        at = (f * ndev + d) * high
+                        to = (f * halves + hh) * high
+                        far_send[d, side, to : to + high] = edge_f[side, hh, at : at + high, :].astype(BF16)
 
     def remote(src, dst, send, recv, where):
         return pltpu.make_async_remote_copy(
             src_ref=src, dst_ref=dst, send_sem=send, recv_sem=recv, device_id=where, device_id_type=MESH
         )
 
-    def left_copy(hh, step):
+    def near_copy(part, hh, step):
+        peer = lax.rem(my_rank + step, team)
+        return remote(
+            near_send.at[part, hh, peer], near_recv.at[part, hh, my_rank],
+            send_n.at[part, hh], recv_n.at[part, hh],
+            (peer // side_cols, my_side * side_cols + lax.rem(peer, side_cols)),
+        )
+
+    def far_copy(step):
         peer, where = other(step)
-        return remote(left_send.at[hh, peer], left_recv.at[hh, me], send_l.at[hh], recv_l.at[hh], where)
-
-    def right_copy(part, step):
-        peer, where = other(step)
-        some = pl.ds(part * each, each)
-        return remote(
-            right_send.at[some, share(peer), :], right_recv.at[part, me],
-            send_r.at[part], recv_r.at[part], where,
-        )
+        return remote(far_send.at[peer], far_recv.at[me], send_f, recv_f, where)
+
+    def near_start(part, hh):
+        with scope("near_start"):
+            near_pack(part, hh)
+            loop(team, lambda step: near_copy(part, hh, step).start())
+            near_recv[part, hh, my_rank] = near_send[part, hh, my_rank]
 
     for hh in range(halves):
-        with scope("edges0"):
-            left_edges(hh)
+        with scope("edges"):
+            edges(hh)
         if hh == 0:
             with scope("barrier"):
                 pl.semaphore_wait(barrier, ndev)
-        with scope("sendl"):
-            loop(ndev, lambda step: left_copy(hh, step).start())
-            left_recv[hh, me] = left_send[hh, me]
-    with scope("edges1"):
-        right_edges()
-    with scope("sendr"):
-        for part in range(parts):
-            loop(ndev, lambda step: right_copy(part, step).start())
-            right_recv[part, me] = right_send[part * each : (part + 1) * each, share(me), :]
+        if parts:
+            near_start(0, hh)
+    with scope("far_start"):
+        far_pack()
+        loop(ndev, lambda step: far_copy(step).start())
+        far_recv[me] = far_send[me]
+    for part in range(1, parts):
+        for hh in range(halves):
+            near_start(part, hh)
     with scope("gate"):
-        for k in (2, 3, 5, 4, 6):
+        for k in (1, 2, 4, 3, 5):
             loads[k].wait()
         tri_out_s[...] = jnp.transpose(tri_out_ref[...].astype(F32)).astype(BF16)
+        tri_gate_t[...] = jnp.transpose(tri_gate_ref[...].astype(F32)).astype(BF16)
         for t in range(tiles):
-            tri_gate_s[t] = jax.nn.sigmoid(
-                lax.dot_general(
-                    tri_gate_ref[...], normed_s[t], (((0,), (1,)), ((), ())), preferred_element_type=F32
-                )
+            gate_t[t] = jax.nn.sigmoid(
+                jnp.dot(tri_gate_t[...], normed_s[t], preferred_element_type=F32)
             )
-            rows = jnp.concatenate([pair_ref[g * tiles + t] for g in range(group)], axis=0)
-            pair_s[t] = jnp.transpose(rows)
     others = pl.ds(0, ndev - 1)
-    with scope("waitl"):
-        for hh in range(halves):
-            arrived(left_recv.at[hh, others], recv_l.at[hh])
+    team_others = pl.ds(0, team - 1)
 
     lane = lax.broadcasted_iota(jnp.int32, (tiles, 128), 1) // cols_dev
 
-    def spread(load, operand):
+    def spread(load, columns, operand):
         for r in range(nrow):
-            for half in range(ncol // group):
-                blocks = [load(r * ncol + half * group + a) for a in range(group)]
+            for half in range(columns // group):
+                blocks = [load(r * columns + half * group + a) for a in range(group)]
                 for b, piece in enumerate(swap_groups(blocks, lane, cols_dev)):
                     operand[
                         pl.ds(r * rows_dev + b * tiles, tiles), pl.ds(half * 128, 128)
                     ] = piece.astype(BF16)
 
-    def prod_copy(part, hh, step):
+    def multiply(left, right, put):
+        products = lax.dot_general(left, right, (((1,), (1,)), ((), ())), preferred_element_type=F32)
+        for r in range(nrow):
+            for half in range(ncol // group):
+                blocks = [
+                    products[
+                        r * rows_dev + a * tiles : r * rows_dev + (a + 1) * tiles,
+                        half * 128 : (half + 1) * 128,
+                    ]
+                    for a in range(group)
+                ]
+                for b, piece in enumerate(swap_groups(blocks, lane, cols_dev)):
+                    for hh in range(halves):
+                        put(r * ncol + half * group + b, hh, piece[hh * high : (hh + 1) * high].astype(BF16))
+
+    def near_pcopy(part, hh, step):
         peer, where = other(step)
-        some = pl.ds(part * each * high, each * high)
         return remote(
-            prod_send.at[peer, hh, some], prod_recv.at[hh, part, me],
-            send_p.at[part, hh], recv_p.at[part, hh], where,
+            near_psend.at[part, hh, peer], near_precv.at[part, hh, me],
+            send_pn.at[part, hh], recv_pn.at[part, hh], where,
         )
 
-    with scope("spreadl"):
-        for c in range(chans):
-            spread(
-                lambda d: jnp.concatenate(
-                    [left_recv[hh, d, c * high : (c + 1) * high].astype(F32) for hh in range(halves)], axis=0
-                ),
-                left_s.at[c],
-            )
+    def far_pcopy(step):
+        peer, where = other(step)
+        return remote(far_psend.at[peer], far_precv.at[me], send_pf, recv_pf, where)
+
+    def near_products(part):
+        for hh in range(halves):
+            with scope("near_wait"):
+                arrived(near_recv.at[part, hh, team_others], recv_n.at[part, hh])
+        with scope("near_products"):
+            for k in range(each):
+                for side, operand in ((0, near_left), (1, near_right)):
+                    spread(
+                        lambda d: jnp.concatenate(
+                            [
+                                near_recv[part, hh, d, side, k * high : (k + 1) * high].astype(F32)
+                                for hh in range(halves)
+                            ],
+                            axis=0,
+                        ),
+                        side_cols, operand.at[k],
+                    )
+
+                def put(d, hh, piece):
+                    near_psend[part, hh, d, k * high : (k + 1) * high] = piece
+
+                multiply(near_left[k], near_right[k], put)
+        with scope("near_psend"):
+            for hh in range(halves):
+                loop(ndev, lambda step: near_pcopy(part, hh, step).start())
+                near_precv[part, hh, me] = near_psend[part, hh, me]
+
+    def far_products():
+        with scope("far_wait"):
+            arrived(far_recv.at[others], recv_f)
+        with scope("far_products"):
+            for f in range(far):
+                for side, operand in ((0, far_left), (1, far_right)):
+                    spread(
+                        lambda d: far_recv[d, side, f * tiles : (f + 1) * tiles].astype(F32), ncol, operand.at[f]
+                    )
+
+                def put(d, hh, piece):
+                    at = (f * halves + hh) * high
+                    far_psend[d, at : at + high] = piece
+
+                multiply(far_left[f], far_right[f], put)
+        with scope("far_psend"):
+            loop(ndev, lambda step: far_pcopy(step).start())
+            far_precv[me] = far_psend[me]
+
     for part in range(parts):
-        with scope("waitr"):
-            arrived(right_recv.at[part, others], recv_r.at[part])
-        with scope("products"):
-            for c in range(part * each, (part + 1) * each):
-                spread(lambda d: right_recv[part, d, c - part * each].astype(F32), right_s.at[c])
-                products = lax.dot_general(
-                    left_s[c], right_s[c], (((1,), (1,)), ((), ())), preferred_element_type=F32
-                )
-                for r in range(nrow):
-                    for half in range(ncol // group):
-                        blocks = [
-                            products[
-                                r * rows_dev + a * tiles : r * rows_dev + (a + 1) * tiles,
-                                half * 128 : (half + 1) * 128,
-                            ]
-                            for a in range(group)
-                        ]
-                        for b, piece in enumerate(swap_groups(blocks, lane, cols_dev)):
-                            for hh in range(halves):
-                                prod_send[r * ncol + half * group + b, hh, c * high : (c + 1) * high] = piece[
-                                    hh * high : (hh + 1) * high
-                                ].astype(BF16)
-        with scope("sendp"):
-            for hh in range(halves if part == parts - 1 else 1):
-                for p in range(part if hh == 0 else 0, part + 1):
-                    loop(ndev, lambda step: prod_copy(p, hh, step).start())
-                    prod_recv[hh, p, me] = prod_send[me, hh, p * each * high : (p + 1) * each * high]
+        if part == 1:
+            far_products()
+        near_products(part)
+    if parts < 2:
+        far_products()
 
     def strip(peer):
         return pl.ds(pl.multiple_of(peer * cols_dev, cols_dev), cols_dev)
@@ -277,20 +332,31 @@
 
     for hh in range(halves):
         with scope("waitp"):
+            if hh == 0:
+                arrived(far_precv.at[others], recv_pf)
             for part in range(parts):
-                arrived(prod_recv.at[hh, part, others], recv_p.at[part, hh])
+                arrived(near_precv.at[part, hh, others], recv_pn.at[part, hh])
         with scope("unpack"):
+            for f in range(far):
+                for d in range(ndev):
+                    at = (f * ndev + d) * high
+                    of = (f * halves + hh) * high
+                    prod_f[at : at + high, :] = far_precv[d, of : of + high].astype(F32)
             for part in range(parts):
-                for d in range(ndev):
-                    for c in range(each):
-                        at = ((part * each + c) * ndev + d) * high
-                        prod_f[at : at + high, :] = prod_recv[hh, part, d, c * high : (c + 1) * high].astype(F32)
+                for rank in range(team):
+                    one = (rank // side_cols) * ncol + rank % side_cols
+                    for k in range(each):
+                        at = near_channel(part * each + k, rank) * high
+                        of = slice(k * high, (k + 1) * high)
+                        prod_f[at : at + high, :] = near_precv[part, hh, one, of].astype(F32) + near_precv[
+                            part, hh, one + side_cols, of
+                        ].astype(F32)
         with scope("middle"):
             for tt in range(high):
                 t = hh * high + tt
                 prods = norm(prod_f[pl.ds(tt, width, stride=high), :], 0).astype(BF16)
                 update = jnp.dot(tri_out_s[...], prods, preferred_element_type=F32)
-                middle = pair_s[t] + tri_gate_s[t] * update
+                middle = pair_s[t] + gate_t[t] * update
                 middle_s[t] = middle
                 normed_mid = norm(middle, 0)
                 own = jnp.dot(bias_w_ref[...], normed_mid.astype(BF16), preferred_element_type=F32)
@@ -440,12 +506,12 @@
         for hh in range(halves):
             run(0, per, lambda i: finish(hh, i))
     with scope("drain"):
-        for hh in range(halves):
-            arrived(left_recv.at[hh, others], send_l.at[hh])
+        arrived(far_recv.at[others], send_f)
+        arrived(far_precv.at[others], send_pf)
         for part in range(parts):
-            arrived(right_recv.at[part, others], send_r.at[part])
             for hh in range(halves):
-                arrived(prod_recv.at[hh, part, others], send_p.at[part, hh])
+                arrived(near_recv.at[part, hh, team_others], send_n.at[part, hh])
+                arrived(near_precv.at[part, hh, others], send_pn.at[part, hh])
         for i in range(per):
             arrived(mid_recv.at[i, pl.ds(0, (ncol - 1) * cols_dev), :], send_m)
             arrived(mid_recv.at[i, pl.ds(0, (ncol - 1) * cols_dev), :], send_g)
@@ -463,8 +529,12 @@
     total = ncol * cols_dev
     tiles = rows_dev // (128 // cols_dev)
     chans = width // ndev
-    parts = 2 if chans % 2 == 0 else 1
-    each = chans // parts
+    far = max(1, chans // 4)
+    near = 2 * (chans - far)
+    parts = 2 if near else 0
+    each = near // 2
+    team = ndev // 2
+    side = ncol // 2 * cols_dev
     per = rows_dev // ncol
     halves = 2 if tiles % 16 == 0 and (tiles // 2) % per == 0 else 1
     high = tiles // halves
@@ -472,30 +542,28 @@
     vmem = pl.BlockSpec(memory_space=pltpu.VMEM)
     held = lambda dtype, *shape: pltpu.VMEM(shape, dtype)
     sem = lambda *shape: pltpu.SemaphoreType.DMA(shape) if shape else pltpu.SemaphoreType.DMA
+    near_held = lambda *shape: held(BF16, *((parts,) + shape if parts else (1, 8, 128)))
+    near_sem = lambda: sem(max(parts, 1), halves)
     bias_w = att_bias.T
     args = [pltpu.with_memory_space_constraint(a, pltpu.HBM) for a in (pair, tri_in, tri_gate, tri_out, att_in, bias_w, att_out)]
     return pl.pallas_call(
-        functools.partial(kernel, (nrow, ncol, rows_dev, cols_dev, width, heads, parts, halves)),
+        functools.partial(kernel, (nrow, ncol, rows_dev, cols_dev, width, heads, far, near, parts, halves)),
         out_shape=jax.ShapeDtypeStruct((rows_dev, cols_dev, width), F32),
         in_specs=[pl.BlockSpec(memory_space=pltpu.SMEM)] + [hbm] * 7,
         out_specs=vmem,
         scratch_shapes=[
             *[held(a.dtype, *a.shape) for a in args],
-            held(BF16, tiles, 128, width),
-            held(F32, 2, width * tiles, 128),
-            held(BF16, halves, ndev, chans * high, 128),
-            held(BF16, chans, ndev * tiles, 128),
-            held(BF16, halves, ndev, chans * high, 128),
-            held(BF16, parts, ndev, each, tiles, 128),
-            held(BF16, chans, total, total),
-            held(BF16, chans, total, total),
-            held(BF16, ndev, halves, chans * high, 128),
-            held(BF16, halves, parts, ndev, each * high, 128),
+            held(BF16, 4 * width, width), held(BF16, width, width), held(BF16, width, width),
+            held(BF16, tiles, width, 128),
+            held(F32, tiles, width, 128), held(F32, tiles, width, 128), held(F32, tiles, width, 128),
+            held(F32, 2, halves, width * high, 128),
+            near_held(halves, team, 2, each * high, 128), near_held(halves, team, 2, each * high, 128),
+            held(BF16, ndev, 2, far * tiles, 128), held(BF16, ndev, 2, far * tiles, 128),
+            held(BF16, max(each, 1), total, side), held(BF16, max(each, 1), total, side),
+            held(BF16, far, total, total), held(BF16, far, total, total),
+            near_held(halves, ndev, each * high, 128), near_held(halves, ndev, each * high, 128),
+            held(BF16, ndev, far * tiles, 128), held(BF16, ndev, far * tiles, 128),
             held(F32, width * high, 128),
-            held(F32, tiles, width, 128),
-            held(F32, tiles, width, 128),
-            held(F32, tiles, width, 128),
-            held(BF16, width, width),
             held(BF16, tiles, 128, width),
             held(BF16, per, total, width),
             held(BF16, per, total, 2 * width),
@@ -506,7 +574,7 @@
             held(F32, halves, heads, total // halves, total),
             held(BF16, halves, per, total // halves, width),
             held(BF16, halves, per, total // halves, width),
-            sem(7), sem(halves), sem(halves), sem(parts), sem(parts), sem(parts, halves), sem(parts, halves),
+            sem(6), sem(halves), near_sem(), near_sem(), sem(), sem(), near_sem(), near_sem(), sem(), sem(),
             sem(), sem(per), sem(3, halves), sem(halves, ncol // 2), sem(3, halves), sem(), sem(halves, per),
         ],
         compiler_params=pltpu.CompilerParams(

time: 69.3 us -> 64.4 us (0.929)
  Pallas kernels: 67.5 us -> 62.6 us
    pallas_call x1, Pallas kernels: 67.5 us -> 62.6 us  [per_device(): pl.pallas_call(functools.partial(kernel, (nrow, ncol, rows_dev, cols_dev,...]
where the time goes in v4:
time: 64.4 us; the launch traced here: 64.2 us
  Pallas kernels  62.6 us (97%)
  local copies, waits for them, and re-layouts  0.97 us (2%)
  between operations  0.66 us (1%)
    pallas_call x1, Pallas kernels, per_device(): pl.pallas_call(functools.partial(kernel, (nrow, ncol, rows_dev, cols_dev,...  62.6 us

profile of v4, /device:TPU:0, one launch (start us, length us, event | category | flops | bytes accessed | tf_op | source)
XLA Modules:
  0.0 64.2 jit_solution(10889631539635546422)
XLA Ops:
  0.7 62.6 %shard_map.82 = f32[64,32,128]{2,1,0:T(8,128)S(1)} custom-call(s32[1]{0:T(128)S(6)} %copy.10.valid_ref, f32[64,32,128]{2,1,0:T(8,128)} %pair_h.1, bf16[128,512]{1,0:T(8,128)(2,1)} %tri_in_h.1, bf16[128,128]{1,0:T(8,128)(2,1)} %tri_gate_h.1, bf16[128,128]{1,0:T(8,128)(2,1)} %tri_out_h.1, bf16[128,512]{1,0:T(8,128)(2,1)} %att_in_h.1, bf16[4,128]{1,0:T(4,128)(2,1)} %bitcast.1, ...), custom_call_target="tpu_custom_call" | custom-call | tf_op jit(solution)/shard_map/pallas_call | solution.py:549
  63.3 1.0 %copy.11 = f32[64,32,128]{2,1,0:T(8,128)} copy(f32[64,32,128]{2,1,0:T(8,128)S(1)} %shard_map.82) | data formatting | bytes 2097152

commit v5 on v4

--- a/solution.py
+++ b/solution.py
@@ -11,6 +11,7 @@
 F32 = jnp.float32
 BF16 = jnp.bfloat16
 scope = jax.named_scope
+PAIR = 2
 
 
 def norm(values, axis):
@@ -46,8 +47,7 @@
     near_psend, near_precv, far_psend, far_precv, prod_f,
     mid_send, mid_recv, kv_s, query_s, gate_s,
     bias_f, bias_recv, bias_full, gated_s, gated_recv,
-    sem_in, sem_pair, send_n, recv_n, send_f, recv_f, send_pn, recv_pn, send_pf, recv_pf, send_m, recv_m,
-    send_b, recv_z, recv_b, send_g, recv_g,
+    sem_in, sem_pair, sent, recv_n, recv_f, recv_pn, recv_pf, recv_m, recv_z, recv_b, recv_g,
 ):
     nrow, ncol, rows_dev, cols_dev, width, heads, far, near, parts, halves = dims
     ndev = nrow * ncol
@@ -129,7 +129,7 @@
             for side in range(2):
                 for k in range(each):
                     at = near_channel(part * each + k, rank) * high
-                    near_send[part, hh, rank, side, k * high : (k + 1) * high] = edge_f[
+                    near_send[part, rank, hh, side, k * high : (k + 1) * high] = edge_f[
                         side, hh, at : at + high, :
                     ].astype(BF16)
 
@@ -142,28 +142,27 @@
                         to = (f * halves + hh) * high
                         far_send[d, side, to : to + high] = edge_f[side, hh, at : at + high, :].astype(BF16)
 
-    def remote(src, dst, send, recv, where):
+    def remote(src, dst, recv, where):
         return pltpu.make_async_remote_copy(
-            src_ref=src, dst_ref=dst, send_sem=send, recv_sem=recv, device_id=where, device_id_type=MESH
+            src_ref=src, dst_ref=dst, send_sem=sent, recv_sem=recv, device_id=where, device_id_type=MESH
         )
 
     def near_copy(part, hh, step):
         peer = lax.rem(my_rank + step, team)
+        some = pl.ds(0, halves) if hh is None else pl.ds(hh, 1)
         return remote(
-            near_send.at[part, hh, peer], near_recv.at[part, hh, my_rank],
-            send_n.at[part, hh], recv_n.at[part, hh],
+            near_send.at[part, peer, some], near_recv.at[part, my_rank, some],
+            recv_n.at[part],
             (peer // side_cols, my_side * side_cols + lax.rem(peer, side_cols)),
         )
 
     def far_copy(step):
         peer, where = other(step)
-        return remote(far_send.at[peer], far_recv.at[me], send_f, recv_f, where)
+        return remote(far_send.at[peer], far_recv.at[me], recv_f, where)
 
     def near_start(part, hh):
         with scope("near_start"):
-            near_pack(part, hh)
             loop(team, lambda step: near_copy(part, hh, step).start())
-            near_recv[part, hh, my_rank] = near_send[part, hh, my_rank]
 
     for hh in range(halves):
         with scope("edges"):
@@ -172,14 +171,20 @@
             with scope("barrier"):
                 pl.semaphore_wait(barrier, ndev)
         if parts:
+            near_pack(0, hh)
             near_start(0, hh)
-    with scope("far_start"):
-        far_pack()
-        loop(ndev, lambda step: far_copy(step).start())
-        far_recv[me] = far_send[me]
+    if far:
+        with scope("far_start"):
+            far_pack()
+            loop(ndev, lambda step: far_copy(step).start())
+            far_recv[me] = far_send[me]
+    for part in range(parts):
+        for hh in range(halves):
+            if part:
+                near_pack(part, hh)
+        near_recv[part, my_rank] = near_send[part, my_rank]
     for part in range(1, parts):
-        for hh in range(halves):
-            near_start(part, hh)
+        near_start(part, None)
     with scope("gate"):
         for k in (1, 2, 4, 3, 5):
             loads[k].wait()
@@ -190,6 +195,10 @@
                 jnp.dot(tri_gate_t[...], normed_s[t], preferred_element_type=F32)
             )
     others = pl.ds(0, ndev - 1)
+    chunks = [(i, 1) for i in range(per)]
+    ready = per // halves
+    waiting = []
+    last = halves - 1
     team_others = pl.ds(0, team - 1)
 
     lane = lax.broadcasted_iota(jnp.int32, (tiles, 128), 1) // cols_dev
@@ -220,26 +229,26 @@
 
     def near_pcopy(part, hh, step):
         peer, where = other(step)
+        some = pl.ds(0, halves) if hh is None else pl.ds(hh, 1)
         return remote(
-            near_psend.at[part, hh, peer], near_precv.at[part, hh, me],
-            send_pn.at[part, hh], recv_pn.at[part, hh], where,
+            near_psend.at[part, peer, some], near_precv.at[part, me, some],
+            recv_pn.at[part + (hh or 0)], where,
         )
 
     def far_pcopy(step):
         peer, where = other(step)
-        return remote(far_psend.at[peer], far_precv.at[me], send_pf, recv_pf, where)
+        return remote(far_psend.at[peer], far_precv.at[me], recv_pf, where)
 
     def near_products(part):
-        for hh in range(halves):
-            with scope("near_wait"):
-                arrived(near_recv.at[part, hh, team_others], recv_n.at[part, hh])
+        with scope("near_wait"):
+            arrived(near_recv.at[part, team_others], recv_n.at[part])
         with scope("near_products"):
             for k in range(each):
                 for side, operand in ((0, near_left), (1, near_right)):
                     spread(
                         lambda d: jnp.concatenate(
                             [
-                                near_recv[part, hh, d, side, k * high : (k + 1) * high].astype(F32)
+                                near_recv[part, d, hh, side, k * high : (k + 1) * high].astype(F32)
                                 for hh in range(halves)
                             ],
                             axis=0,
@@ -248,13 +257,13 @@
                     )
 
                 def put(d, hh, piece):
-                    near_psend[part, hh, d, k * high : (k + 1) * high] = piece
+                    near_psend[part, d, hh, k * high : (k + 1) * high] = piece
 
                 multiply(near_left[k], near_right[k], put)
         with scope("near_psend"):
-            for hh in range(halves):
+            for hh in range(halves) if part == parts - 1 else (None,):
                 loop(ndev, lambda step: near_pcopy(part, hh, step).start())
-                near_precv[part, hh, me] = near_psend[part, hh, me]
+            near_precv[part, me] = near_psend[part, me]
 
     def far_products():
         with scope("far_wait"):
@@ -276,7 +285,7 @@
             far_precv[me] = far_psend[me]
 
     for part in range(parts):
-        if part == 1:
+        if part == 1 and far:
             far_products()
         near_products(part)
     if parts < 2:
@@ -285,57 +294,63 @@
     def strip(peer):
         return pl.ds(pl.multiple_of(peer * cols_dev, cols_dev), cols_dev)
 
-    def send_rows(t):
-        i = t // span
-        for g in range(group):
-            turn = lax.rem(g + my_z, group)
-            owner = turn * span + t % span
-
-            @pl.when(owner != my_col)
-            def _():
-                remote(
-                    mid_send.at[t, strip(turn), :], mid_recv.at[i, strip(my_col), :],
-                    send_m, recv_m.at[i], (my_row, owner),
-                ).start()
-
-            @pl.when(owner == my_col)
-            def _():
-                mid_recv[i, strip(my_col), :] = mid_send[t, strip(turn), :]
+    def send_rows(chunk, steps):
+        first, count = chunks[chunk]
+        some = pl.ds(first, count)
+        for step in steps:
+            peer = lax.rem(my_col + step, ncol)
+            remote(
+                mid_send.at[peer, some], mid_recv.at[some, strip(my_col), :],
+                recv_m.at[first // PAIR], (my_row, peer),
+            ).start()
+
+    def keep_rows(chunk):
+        first, count = chunks[chunk]
+        for i in range(first, first + count):
+            mid_recv[i, strip(my_col), :] = mid_send[my_col, i]
 
     def bias_block(hh, z):
         block = bias_recv.at[core, hh, my_row, z]
         for step in range(1, nrow):
             peer = lax.rem(my_row + step, nrow)
-            remote(block, block, send_b.at[1, hh], recv_b.at[1, hh], (peer, my_col)).start()
+            remote(block, block, recv_b.at[0, hh], (peer, my_col)).start()
 
     def bias_z(hh):
         mine = bias_recv.at[core, hh, my_row, my_z]
         for step in range(1, nz):
             peer = lax.rem(my_z + step, nz)
-            remote(mine, mine, send_b.at[0, hh], recv_z.at[hh, my_z], (my_row, 2 * peer + core)).start()
-        bias_block(hh, my_z)
+            remote(mine, mine, recv_z.at[hh if hh < last else last + my_z], (my_row, 2 * peer + core)).start()
+        if hh == last:
+            bias_block(hh, my_z)
 
     def bias_row(hh):
+        if hh < last:
+            arrived(bias_recv.at[0, hh, 0, pl.ds(0, nz - 1)], recv_z.at[hh])
+            bias_block(hh, slice(None))
+            return
         turn = 1 - 2 * (my_z // (nz // 2))
         for step in range(1, nz):
             z = lax.rem(my_z + turn * step + nz, nz)
-            arrived(bias_recv.at[0, hh, 0, 0], recv_z.at[hh, z])
+            arrived(bias_recv.at[0, hh, 0, 0], recv_z.at[last + z])
             bias_block(hh, z)
 
     def bias_hand(hh):
         mine = bias_recv.at[core, hh]
-        return remote(mine, mine, send_b.at[2, hh], recv_b.at[2, hh], (my_row, my_col + 1 - 2 * core))
+        return remote(mine, mine, recv_b.at[1, hh], (my_row, my_col + 1 - 2 * core))
 
     def bias_core(hh):
-        arrived(bias_recv.at[0, hh, pl.ds(0, nrow - 1)], recv_b.at[1, hh])
+        arrived(bias_recv.at[0, hh, pl.ds(0, nrow - 1)], recv_b.at[0, hh])
         bias_hand(hh).start()
 
     for hh in range(halves):
         with scope("waitp"):
             if hh == 0:
-                arrived(far_precv.at[others], recv_pf)
-            for part in range(parts):
-                arrived(near_precv.at[part, hh, others], recv_pn.at[part, hh])
+                if far:
+                    arrived(far_precv.at[others], recv_pf)
+                for part in range(parts - 1):
+                    arrived(near_precv.at[part, others], recv_pn.at[part])
+            if parts:
+                arrived(near_precv.at[parts - 1, others, hh], recv_pn.at[parts - 1 + hh])
         with scope("unpack"):
             for f in range(far):
                 for d in range(ndev):
@@ -348,8 +363,8 @@
                     for k in range(each):
                         at = near_channel(part * each + k, rank) * high
                         of = slice(k * high, (k + 1) * high)
-                        prod_f[at : at + high, :] = near_precv[part, hh, one, of].astype(F32) + near_precv[
-                            part, hh, one + side_cols, of
+                        prod_f[at : at + high, :] = near_precv[part, one, hh, of].astype(F32) + near_precv[
+                            part, one + side_cols, hh, of
                         ].astype(F32)
         with scope("middle"):
             for tt in range(high):
@@ -362,27 +377,30 @@
                 own = jnp.dot(bias_w_ref[...], normed_mid.astype(BF16), preferred_element_type=F32)
                 for h in range(heads):
                     bias_f[pl.ds(h * high + tt, 1), :] = own[h : h + 1]
-                mid_send[t] = jnp.transpose(normed_mid).astype(BF16)
+                normed_mid = jnp.transpose(normed_mid).astype(BF16)
+                for g in range(group):
+                    mid_send[g * span + t % span, t // span] = normed_mid[g * cols_dev : (g + 1) * cols_dev]
         with scope("bias_z"):
             bias_recv[core, hh, my_row, my_z] = bias_f[...].astype(BF16)
             bias_z(hh)
         with scope("send_rows"):
-            early = range(3 * high // 4) if hh == 0 and halves > 1 else range(high)
-            if hh > 0:
-                for tt in range(3 * high // 4 if hh == 1 else high, high):
-                    send_rows((hh - 1) * high + tt)
-            for tt in early:
-                send_rows(hh * high + tt)
+            fresh = [chunk for chunk, (first, _) in enumerate(chunks) if first // ready == hh]
+            held = max(1, len(fresh) // 4) if hh < halves - 1 else 0
+            for chunk in waiting + fresh[: len(fresh) - held]:
+                send_rows(chunk, range(1, ncol))
+                keep_rows(chunk)
+            waiting = fresh[len(fresh) - held :]
 
     def take(i):
-        arrived(mid_recv.at[i, pl.ds(0, (ncol - 1) * cols_dev), :], recv_m.at[i])
+        if i % PAIR == 0:
+            arrived(mid_recv.at[pl.ds(i, PAIR), pl.ds(0, (ncol - 1) * cols_dev), :], recv_m.at[i // PAIR])
 
     tokens = lax.broadcasted_iota(jnp.int32, (1, total), 1)
     mask = jnp.where(tokens < valid, 0.0, -1000000000.0)
     narrow = lax.broadcasted_iota(jnp.int32, (high, 128), 1) // cols_dev
 
     def assemble(hh):
-        arrived(bias_recv.at[0, hh], recv_b.at[2, hh])
+        arrived(bias_recv.at[0, hh], recv_b.at[1, hh])
         for h in range(heads):
             for r in range(nrow):
                 for half in range(ncol // group):
@@ -433,7 +451,7 @@
         peer = lax.rem(my_col + step, ncol)
         return remote(
             gated_s.at[hh, i, share_cols(peer), :], gated_recv.at[hh, i, share_cols(my_col), :],
-            send_g, recv_g.at[hh, i], (my_row, peer),
+            recv_g.at[hh if hh < last else last + i], (my_row, peer),
         )
 
     def attend(hh, i):
@@ -471,7 +489,6 @@
         project(i)
         attend(0, i)
 
-    ready = per // halves
     project(0)
     with scope("bias_row"):
         for hh in range(1, halves):
@@ -480,12 +497,14 @@
         assemble(0)
     with scope("attend"):
         attend(0, 0)
-        run(1, ready, first_pass)
+        for i in range(1, ready):
+            first_pass(i)
     with scope("bias_core"):
         for hh in range(1, halves):
             bias_core(hh)
     with scope("attend"):
-        run(ready, per, first_pass)
+        for i in range(ready, per):
+            first_pass(i)
     for hh in range(1, halves):
         with scope("assemble"):
             assemble(hh)
@@ -493,8 +512,9 @@
             run(0, per, lambda i: attend(hh, i))
 
     def finish(hh, i):
-        with scope("waitg"):
-            arrived(gated_recv.at[hh, i, pl.ds(0, (ncol - 1) * own_cols), :], recv_g.at[hh, i])
+        if hh == last:
+            with scope("waitg"):
+                arrived(gated_recv.at[hh, i, pl.ds(0, (ncol - 1) * own_cols), :], recv_g.at[last + i])
         added = jnp.dot(gated_recv[hh, i], att_out_ref[...], preferred_element_type=F32)
         for q in range(ncol):
             row = (q // span) * tiles + i * span + q % span
@@ -504,21 +524,22 @@
 
     with scope("finish"):
         for hh in range(halves):
+            if hh < last:
+                arrived(gated_recv.at[hh, :, pl.ds(0, (ncol - 1) * own_cols), :], recv_g.at[hh])
             run(0, per, lambda i: finish(hh, i))
     with scope("drain"):
-        arrived(far_recv.at[others], send_f)
-        arrived(far_precv.at[others], send_pf)
+        arrived(far_recv.at[others], sent)
+        arrived(far_precv.at[others], sent)
         for part in range(parts):
+            arrived(near_recv.at[part, team_others], sent)
             for hh in range(halves):
-                arrived(near_recv.at[part, hh, team_others], send_n.at[part, hh])
-                arrived(near_precv.at[part, hh, others], send_pn.at[part, hh])
-        for i in range(per):
-            arrived(mid_recv.at[i, pl.ds(0, (ncol - 1) * cols_dev), :], send_m)
-            arrived(mid_recv.at[i, pl.ds(0, (ncol - 1) * cols_dev), :], send_g)
+                arrived(near_precv.at[part, others, hh], sent)
+        arrived(mid_recv.at[:, pl.ds(0, (ncol - 1) * cols_dev), :], sent)
         for hh in range(halves):
-            arrived(bias_recv.at[0, hh, 0, pl.ds(0, nz - 1)], send_b.at[0, hh])
-            arrived(bias_recv.at[0, hh, pl.ds(0, nrow - 1)], send_b.at[1, hh])
-            arrived(bias_recv.at[0, hh], send_b.at[2, hh])
+            arrived(gated_recv.at[hh, :, pl.ds(0, (ncol - 1) * own_cols), :], sent)
+            arrived(bias_recv.at[0, hh, 0, pl.ds(0, nz - 1)], sent)
+            arrived(bias_recv.at[0, hh, pl.ds(0, nrow - 1)], sent)
+            arrived(bias_recv.at[0, hh], sent)
 
 
 def per_device(pair, valid_length, tri_in, tri_gate, tri_out, att_in, att_bias, att_out):
@@ -539,32 +560,30 @@
     halves = 2 if tiles % 16 == 0 and (tiles // 2) % per == 0 else 1
     high = tiles // halves
     hbm = pl.BlockSpec(memory_space=pltpu.HBM)
-    vmem = pl.BlockSpec(memory_space=pltpu.VMEM)
     held = lambda dtype, *shape: pltpu.VMEM(shape, dtype)
     sem = lambda *shape: pltpu.SemaphoreType.DMA(shape) if shape else pltpu.SemaphoreType.DMA
     near_held = lambda *shape: held(BF16, *((parts,) + shape if parts else (1, 8, 128)))
-    near_sem = lambda: sem(max(parts, 1), halves)
     bias_w = att_bias.T
     args = [pltpu.with_memory_space_constraint(a, pltpu.HBM) for a in (pair, tri_in, tri_gate, tri_out, att_in, bias_w, att_out)]
     return pl.pallas_call(
         functools.partial(kernel, (nrow, ncol, rows_dev, cols_dev, width, heads, far, near, parts, halves)),
         out_shape=jax.ShapeDtypeStruct((rows_dev, cols_dev, width), F32),
         in_specs=[pl.BlockSpec(memory_space=pltpu.SMEM)] + [hbm] * 7,
-        out_specs=vmem,
+        out_specs=pl.BlockSpec(memory_space=pltpu.VMEM),
         scratch_shapes=[
             *[held(a.dtype, *a.shape) for a in args],
             held(BF16, 4 * width, width), held(BF16, width, width), held(BF16, width, width),
             held(BF16, tiles, width, 128),
             held(F32, tiles, width, 128), held(F32, tiles, width, 128), held(F32, tiles, width, 128),
             held(F32, 2, halves, width * high, 128),
-            near_held(halves, team, 2, each * high, 128), near_held(halves, team, 2, each * high, 128),
-            held(BF16, ndev, 2, far * tiles, 128), held(BF16, ndev, 2, far * tiles, 128),
+            near_held(team, halves, 2, each * high, 128), near_held(team, halves, 2, each * high, 128),
+            held(BF16, ndev, 2, max(far, 1) * tiles, 128), held(BF16, ndev, 2, max(far, 1) * tiles, 128),
             held(BF16, max(each, 1), total, side), held(BF16, max(each, 1), total, side),
-            held(BF16, far, total, total), held(BF16, far, total, total),
-            near_held(halves, ndev, each * high, 128), near_held(halves, ndev, each * high, 128),
-            held(BF16, ndev, far * tiles, 128), held(BF16, ndev, far * tiles, 128),
+            held(BF16, max(far, 1), total, total), held(BF16, max(far, 1), total, total),
+            near_held(ndev, halves, each * high, 128), near_held(ndev, halves, each * high, 128),
+            held(BF16, ndev, max(far, 1) * tiles, 128), held(BF16, ndev, max(far, 1) * tiles, 128),
             held(F32, width * high, 128),
-            held(BF16, tiles, 128, width),
+            held(BF16, ncol, per, cols_dev, width),
             held(BF16, per, total, width),
             held(BF16, per, total, 2 * width),
             held(BF16, per, halves, total // halves, width),
@@ -574,8 +593,8 @@
             held(F32, halves, heads, total // halves, total),
             held(BF16, halves, per, total // halves, width),
             held(BF16, halves, per, total // halves, width),
-            sem(6), sem(halves), near_sem(), near_sem(), sem(), sem(), near_sem(), near_sem(), sem(), sem(),
-            sem(), sem(per), sem(3, halves), sem(halves, ncol // 2), sem(3, halves), sem(), sem(halves, per),
+            sem(6), sem(halves), sem(), sem(max(parts, 1)), sem(), sem(max(parts, 1) + halves), sem(),
+            sem(per // PAIR), sem(halves + ncol // 2), sem(2, halves), sem(halves + per),
         ],
         compiler_params=pltpu.CompilerParams(
             collective_id=0, has_side_effects=True, vmem_limit_bytes=40 * 1024 * 1024

time: 64.4 us -> 64.2 us (level)
  no operation moved by 1% of the time
where the time goes in v5:
time: 64.2 us; the launch traced here: 64 us
  Pallas kernels  62.4 us (97%)
  local copies, waits for them, and re-layouts  0.97 us (2%)
  between operations  0.66 us (1%)
    pallas_call x1, Pallas kernels, per_device(): pl.pallas_call(functools.partial(kernel, (nrow, ncol, rows_dev, cols_dev,...  62.4 us

profile of v5, /device:TPU:0, one launch (start us, length us, event | category | flops | bytes accessed | tf_op | source)
XLA Modules:
  0.0 64.0 jit_solution(16927324900675764000)
XLA Ops:
  0.7 62.4 %shard_map.82 = f32[64,32,128]{2,1,0:T(8,128)S(1)} custom-call(s32[1]{0:T(128)S(6)} %copy.10.valid_ref, f32[64,32,128]{2,1,0:T(8,128)} %pair_h.1, bf16[128,512]{1,0:T(8,128)(2,1)} %tri_in_h.1, bf16[128,128]{1,0:T(8,128)(2,1)} %tri_gate_h.1, bf16[128,128]{1,0:T(8,128)(2,1)} %tri_out_h.1, bf16[128,512]{1,0:T(8,128)(2,1)} %att_in_h.1, bf16[4,128]{1,0:T(4,128)(2,1)} %bitcast.1, ...), custom_call_target="tpu_custom_call" | custom-call | tf_op jit(solution)/shard_map/pallas_call | solution.py:568
  63.0 1.0 %copy.11 = f32[64,32,128]{2,1,0:T(8,128)} copy(f32[64,32,128]{2,1,0:T(8,128)S(1)} %shard_map.82) | data formatting | bytes 2097152

commit v6 on v5

--- a/solution.py
+++ b/solution.py
@@ -39,9 +39,9 @@
 
 def kernel(
     dims,
-    valid_ref, pair_h, tri_in_h, tri_gate_h, tri_out_h, att_in_h, bias_w_h, att_out_h,
+    valid_h, pair_h, tri_in_h, tri_gate_h, tri_out_h, att_in_h, bias_w_h, att_out_h,
     out_ref,
-    pair_ref, tri_in_ref, tri_gate_ref, tri_out_ref, att_in_ref, bias_w_ref, att_out_ref,
+    valid_ref, pair_ref, tri_in_ref, tri_gate_ref, tri_out_ref, att_in_ref, bias_w_ref, att_out_ref,
     tri_in_s, tri_gate_t, tri_out_s, normed_s, pair_s, middle_s, gate_t, edge_f,
     near_send, near_recv, far_send, far_recv, near_left, near_right, far_left, far_right,
     near_psend, near_precv, far_psend, far_precv, prod_f,
@@ -67,10 +67,11 @@
     core, my_z = lax.rem(my_col, 2), my_col // 2
     my_side, my_rank = my_col // side_cols, my_row * side_cols + lax.rem(my_col, side_cols)
 
-    held = (tri_in_ref, tri_gate_ref, tri_out_ref, att_in_ref, bias_w_ref, att_out_ref)
-    given = (tri_in_h, tri_gate_h, tri_out_h, att_in_h, bias_w_h, att_out_h)
+    held = (tri_in_ref, tri_gate_ref, tri_out_ref, att_in_ref, bias_w_ref, att_out_ref, valid_ref)
+    given = (tri_in_h, tri_gate_h, tri_out_h, att_in_h, bias_w_h, att_out_h, valid_h)
     loads = [pltpu.make_async_copy(g, v, sem_in.at[k]) for k, (g, v) in enumerate(zip(given, held))]
     loads[0].start()
+    loads[6].start()
     for hh in range(halves):
         for g in range(group):
             some = pl.ds(g * tiles + hh * high, high)
@@ -96,8 +97,9 @@
                 pl.semaphore_signal(barrier, inc=1, device_id=(r, c), device_id_type=MESH)
     with scope("inputs"):
         loads[0].wait()
+        loads[6].wait()
         tri_in_s[...] = jnp.transpose(tri_in_ref[...].astype(F32)).astype(BF16)
-    valid = valid_ref[0]
+    valid = valid_ref[...]
 
     lanes = lax.broadcasted_iota(jnp.int32, (1, 128), 1)
     lane_col = my_col * cols_dev + lanes % cols_dev
@@ -447,12 +449,14 @@
     def share_cols(peer):
         return pl.ds(pl.multiple_of(peer * own_cols, own_cols), own_cols)
 
-    def home_copy(hh, i, step):
-        peer = lax.rem(my_col + step, ncol)
-        return remote(
-            gated_s.at[hh, i, share_cols(peer), :], gated_recv.at[hh, i, share_cols(my_col), :],
-            recv_g.at[hh if hh < last else last + i], (my_row, peer),
-        )
+    def send_home(hh, first, count):
+        some = pl.ds(first, count)
+        for step in range(1, ncol):
+            peer = lax.rem(my_col + step, ncol)
+            remote(
+                gated_s.at[hh, some, share_cols(peer), :], gated_recv.at[hh, some, share_cols(my_col), :],
+                recv_g.at[hh if hh < last else last + first // PAIR], (my_row, peer),
+            ).start()
 
     def attend(hh, i):
         keys = kv_s[i, :, :width]
@@ -474,9 +478,15 @@
             gated_s[hh, i, first : first + block, :] = (
                 gate_s[i, hh, first : first + block, :] * top / bottom
             ).astype(BF16)
-        for step in range(1, ncol):
-            home_copy(hh, i, step).start()
-        gated_recv[hh, i, share_cols(my_col), :] = gated_s[hh, i, share_cols(my_col), :]
+
+    def attend_batch(hh, first):
+        for k in range(ready):
+            attend(hh, first + k)
+        size = ready if hh < last else PAIR
+        for k in range(0, ready, size):
+            send_home(hh, first + k, size)
+        for k in range(ready):
+            gated_recv[hh, first + k, share_cols(my_col), :] = gated_s[hh, first + k, share_cols(my_col), :]
 
     def run(first, last, act):
         def body(i, carry):
@@ -485,36 +495,39 @@
 
         lax.fori_loop(first, last, body, 0)
 
-    def first_pass(i):
+    for i in range(min(PAIR, ready)):
         project(i)
-        attend(0, i)
-
-    project(0)
     with scope("bias_row"):
         for hh in range(1, halves):
             bias_row(hh)
+    for i in range(PAIR, ready):
+        project(i)
     with scope("assemble"):
         assemble(0)
     with scope("attend"):
-        attend(0, 0)
-        for i in range(1, ready):
-            first_pass(i)
+        attend_batch(0, 0)
     with scope("bias_core"):
         for hh in range(1, halves):
             bias_core(hh)
-    with scope("attend"):
-        for i in range(ready, per):
-            first_pass(i)
+    for first in range(ready, per, ready):
+        for i in range(first, first + ready):
+            project(i)
+        with scope("attend"):
+            attend_batch(0, first)
     for hh in range(1, halves):
         with scope("assemble"):
             assemble(hh)
         with scope("attend"):
-            run(0, per, lambda i: attend(hh, i))
+            run(0, per // ready, lambda k: attend_batch(hh, k * ready))
 
     def finish(hh, i):
         if hh == last:
-            with scope("waitg"):
-                arrived(gated_recv.at[hh, i, pl.ds(0, (ncol - 1) * own_cols), :], recv_g.at[last + i])
+            if i % PAIR == 0:
+                with scope("waitg"):
+                    arrived(
+                        gated_recv.at[hh, pl.ds(i, PAIR), pl.ds(0, (ncol - 1) * own_cols), :],
+                        recv_g.at[last + i // PAIR],
+                    )
         added = jnp.dot(gated_recv[hh, i], att_out_ref[...], preferred_element_type=F32)
         for q in range(ncol):
             row = (q // span) * tiles + i * span + q % span
@@ -526,7 +539,8 @@
         for hh in range(halves):
             if hh < last:
                 arrived(gated_recv.at[hh, :, pl.ds(0, (ncol - 1) * own_cols), :], recv_g.at[hh])
-            run(0, per, lambda i: finish(hh, i))
+            for i in range(per):
+                finish(hh, i)
     with scope("drain"):
         arrived(far_recv.at[others], sent)
         arrived(far_precv.at[others], sent)
@@ -568,9 +582,10 @@
     return pl.pallas_call(
         functools.partial(kernel, (nrow, ncol, rows_dev, cols_dev, width, heads, far, near, parts, halves)),
         out_shape=jax.ShapeDtypeStruct((rows_dev, cols_dev, width), F32),
-        in_specs=[pl.BlockSpec(memory_space=pltpu.SMEM)] + [hbm] * 7,
+        in_specs=[pl.BlockSpec(memory_space=pl.ANY)] + [hbm] * 7,
         out_specs=pl.BlockSpec(memory_space=pltpu.VMEM),
         scratch_shapes=[
+            held(jnp.int32, 1, 1),
             *[held(a.dtype, *a.shape) for a in args],
             held(BF16, 4 * width, width), held(BF16, width, width), held(BF16, width, width),
             held(BF16, tiles, width, 128),
@@ -593,13 +608,13 @@
             held(F32, halves, heads, total // halves, total),
             held(BF16, halves, per, total // halves, width),
             held(BF16, halves, per, total // halves, width),
-            sem(6), sem(halves), sem(), sem(max(parts, 1)), sem(), sem(max(parts, 1) + halves), sem(),
-            sem(per // PAIR), sem(halves + ncol // 2), sem(2, halves), sem(halves + per),
+            sem(7), sem(halves), sem(), sem(max(parts, 1)), sem(), sem(max(parts, 1) + halves), sem(),
+            sem(per // PAIR), sem(halves + ncol // 2), sem(2, halves), sem(halves + per // PAIR),
         ],
         compiler_params=pltpu.CompilerParams(
             collective_id=0, has_side_effects=True, vmem_limit_bytes=40 * 1024 * 1024
         ),
-    )(valid_length, *args)
+    )(valid_length.reshape(1, 1), *args)
 
 
 def solution(mesh):

time: 64.2 us -> 64.1 us (level)
  no operation moved by 1% of the time
where the time goes in v6:
time: 64.1 us; the launch traced here: 64 us
  Pallas kernels  62.3 us (97%)
  local copies, waits for them, and re-layouts  0.97 us (2%)
  between operations  0.66 us (1%)
    pallas_call x1, Pallas kernels, per_device(): pl.pallas_call(functools.partial(kernel, (nrow, ncol, rows_dev, cols_dev,...  62.3 us

profile of v6, /device:TPU:0, one launch (start us, length us, event | category | flops | bytes accessed | tf_op | source)
XLA Modules:
  0.0 64.0 jit_solution(315314348231811346)
XLA Ops:
  0.7 62.3 %shard_map.82 = f32[64,32,128]{2,1,0:T(8,128)S(1)} custom-call(s32[1,1]{1,0:T(1,128)} %bitcast.2.valid_h, f32[64,32,128]{2,1,0:T(8,128)} %pair_h.1, bf16[128,512]{1,0:T(8,128)(2,1)} %tri_in_h.1, bf16[128,128]{1,0:T(8,128)(2,1)} %tri_gate_h.1, bf16[128,128]{1,0:T(8,128)(2,1)} %tri_out_h.1, bf16[128,512]{1,0:T(8,128)(2,1)} %att_in_h.1, ...), custom_call_target="tpu_custom_call" | custom-call | tf_op jit(solution)/shard_map/pallas_call | solution.py:582
  63.0 1.0 %copy.11 = f32[64,32,128]{2,1,0:T(8,128)} copy(f32[64,32,128]{2,1,0:T(8,128)S(1)} %shard_map.82) | data formatting | bytes 2097152
